TPU v7x, 32 devices: a whole 2x2x4 slice. The times are simulated.
32 devices in a mesh: leaf: 4 (over x, core), blk: 8 (over z, y).
Axes of the slice: x: 2, y: 2, z: 4, core: 2. Of those that a mesh axis runs over, the one named last changes fastest.
Arguments:
- right_side: float32 [4, 4, 8, 384], P(None, 'leaf', 'blk'), may hold values from -6 to 6
- diag_inverse: bfloat16 [4, 8, 128, 7168], P('leaf', 'blk'), as said below
- update_factor: bfloat16 [4, 8, 128, 10240], P('leaf', 'blk'), may hold values from -0.09375 to 0.09375
- live_blocks: int32 [7], replicated, may hold values from 1 to 32, as said below
Outputs:
- forward_solution: float32 [4, 4, 8, 384], P(None, 'leaf', 'blk')
- solution: float32 [4, 4, 8, 384], P(None, 'leaf', 'blk')
Inputs may be any that keep to these rules, and one draw needn't show every extreme that they name: `live_blocks`: A supernode with 2^l * 8 block-rows (level l, listed level by level from level 0, by group within a level) has between a quarter of them (at least 1) and all of them live; the root supernode (the last entry) has all of them live. `diag_inverse`: each level's inverse diagonal block is lower triangular in its supernode's row order, with a positive diagonal.
All inputs are finite; a program needn't handle non-finite values.
Results may differ from a plain program's by a relative error of at most 0.009.
Values sent between devices are 32-bit elements; how exact they have to be, the bound alone decides.
No kernel may reach another device: no remote copies, remote signals or barrier semaphores. Data moves between devices by JAX's collectives and lax.ppermute only.
A program may use at most 128 MiB of HBM per device.

v0:
```python
import jax
import jax.numpy as jnp
from jax import lax
from jax.sharding import PartitionSpec as P


def swapped(block, axis, apart):
    count = lax.axis_size(axis)
    route = []
    for low in range(count):
        high = low | 1 << apart
        if high != low and high < count:
            route += [(low, high), (high, low)]
    return lax.ppermute(block, axis, route)


def group_sum(partial_value, height):
    current = lax.psum(partial_value, "blk")
    for bit_number in range(height):
        current = current + swapped(current, "leaf", bit_number)
    return current


def local(right_side, diag_inverse, update_factor, live_blocks):
    leaf_count = lax.axis_size("leaf")
    block_count = lax.axis_size("blk")
    levels = leaf_count.bit_length()
    leaf_index = lax.axis_index("leaf")
    block_index = lax.axis_index("blk")
    block_rows = diag_inverse.shape[2]
    vectors = right_side.shape[0]
    level_width = block_count * block_rows
    rows_all = leaf_count * level_width
    flat_side = right_side.reshape(vectors, 1, levels * block_rows)
    every_side = lax.all_gather(flat_side, ("leaf", "blk"), axis=1, tiled=True)
    inverse_rows = diag_inverse.reshape(block_rows, -1)
    update_rows = update_factor.reshape(block_rows, -1)
    orders = [(1 << height) * level_width for height in range(levels)]
    spans = [sum(orders[height + 1 :]) for height in range(levels)]
    update_start = [sum(spans[:height]) for height in range(levels)]
    contract_second = (((1,), (1,)), ((), ()))
    own_masks = []
    group_masks = []
    own_starts = []
    group_starts = []
    inverse_parts = []
    update_parts = []
    for height in range(levels):
        group_index = leaf_index >> height
        local_rank = leaf_index & (1 << height) - 1
        offset = 2 * leaf_count - (2 * leaf_count >> height)
        live_count = live_blocks[offset + group_index]
        own_position = local_rank * block_count + block_index
        own_masks.append((own_position < live_count).astype(jnp.float32))
        block_alive = (jnp.arange((1 << height) * block_count) < live_count).astype(jnp.float32)
        group_masks.append(jnp.repeat(block_alive, block_rows))
        own_starts.append(own_position * block_rows)
        group_starts.append(group_index * orders[height])
        start = ((1 << height) - 1) * level_width
        inverse_parts.append(inverse_rows[:, start : start + orders[height]])
        update_parts.append(
            update_rows[:, update_start[height] : update_start[height] + spans[height]]
        )
    pending = [jnp.zeros((vectors, orders[height]), jnp.float32) for height in range(levels)]
    forward = []
    for height in range(levels):
        level_side = every_side[:, :, height * block_rows : (height + 1) * block_rows].reshape(
            vectors, rows_all
        )
        source = lax.dynamic_slice_in_dim(level_side, group_starts[height], orders[height], 1)
        if height > 0:
            source = source - group_sum(pending[height], height)
        reduced = (group_masks[height] * source).astype(jnp.bfloat16)
        solved = own_masks[height] * lax.dot_general(
            reduced, inverse_parts[height], contract_second, preferred_element_type=jnp.float32
        )
        forward.append(solved)
        if height < levels - 1:
            spread = jnp.dot(
                solved.astype(jnp.bfloat16),
                update_parts[height],
                preferred_element_type=jnp.float32,
            )
            cursor = 0
            for ancestor in range(height + 1, levels):
                pending[ancestor] = (
                    pending[ancestor] + spread[:, cursor : cursor + orders[ancestor]]
                )
                cursor += orders[ancestor]
    whole_solved = [None] * levels
    backward = [None] * levels
    for height in reversed(range(levels)):
        residual = forward[height]
        if height < levels - 1:
            ancestors = jnp.concatenate(
                [whole_solved[ancestor] for ancestor in range(height + 1, levels)], axis=1
            )
            residual = residual - lax.dot_general(
                ancestors, update_parts[height], contract_second, preferred_element_type=jnp.float32
            )
        weighted = (own_masks[height] * residual).astype(jnp.bfloat16)
        partial_value = jnp.dot(weighted, inverse_parts[height], preferred_element_type=jnp.float32)
        supernode_solved = group_masks[height] * group_sum(partial_value, height)
        backward[height] = lax.dynamic_slice_in_dim(
            supernode_solved, own_starts[height], block_rows, 1
        )
        whole_solved[height] = supernode_solved.astype(jnp.bfloat16)
    forward_out = jnp.stack(forward, axis=1).reshape(vectors, 1, 1, levels * block_rows)
    backward_out = jnp.stack(backward, axis=1).reshape(vectors, 1, 1, levels * block_rows)
    return (forward_out, backward_out)


def solution(mesh):
    in_specs = (
        P(None, "leaf", "blk", None),
        P("leaf", "blk", None, None),
        P("leaf", "blk", None, None),
        P(),
    )
    out_specs = (P(None, "leaf", "blk", None), P(None, "leaf", "blk", None))
    return jax.shard_map(local, mesh=mesh, in_specs=in_specs, out_specs=out_specs, check_vma=False)
```

profile of v0, /device:TPU:0, one launch (start us, length us, event | category | flops | bytes accessed | tf_op | source)
XLA Modules:
  0.0 352.7 jit_solution(483365086368205140)
XLA Ops:
  7.2 0.0 copy-start
  7.2 0.0 all-reduce.3.cloned.1.call-start
  7.2 71.2 %all-gather = f32[4,32,1,384]{3,2,1,0:T(1,128)S(1)} all-gather(f32[4,1,1,384]{3,2,1,0:T(1,128)} %param.4), channel_id=2, replica_groups=mesh['leaf'=4,'blk'=8] {'leaf','blk'}, dimensions={1}, use_global_device_ids=true | all-gather | bytes 202752 | tf_op jit(solution)/shard_map/all_gather | solution.py:35
  78.5 1.4 fusion.53
  80.0 0.6 compare_convert_fusion.2
  80.6 0.1 broadcast_bitcast_fusion.2
  81.3 1.1 convolution_multiply_fusion.1
  82.5 1.7 fusion.2
  84.2 33.0 %psum.35 = f32[4,2048]{1,0:T(4,128)S(1)} all-reduce(f32[4,2048]{1,0:T(4,128)S(1)} %slice.44), channel_id=1, replica_groups=mesh['leaf'=4,'blk'=8] {'blk'}, use_global_device_ids=true, to_apply=%region_0.0 | all-reduce | flops 8192 | bytes 65536 | tf_op jit(solution)/shard_map/psum | solution.py:18
  117.2 0.0 collective-permute-start
  117.2 0.6 compare_convert_fusion.1
  117.9 0.1 broadcast_bitcast_fusion.1
  118.6 0.0 collective-permute-done
  118.6 0.0 copy-done
  118.6 0.2 convolution_multiply_fusion.2
  118.9 2.1 convolution_add_fusion
  121.0 0.0 all-reduce.3.cloned.1.call-update
  121.0 0.0 all-reduce.5.cloned.1.call-start
  121.1 65.9 %all-reduce.3.cloned.1.call-done = f32[4,4096]{1,0:T(4,128)} async-done(((f32[4,4096]{1,0:T(4,128)}), f32[4,4096]{1,0:T(4,128)}) %all-reduce.3.cloned.1.call-update) | async-done | bytes 65552 | tf_op jit(solution)/shard_map/psum | solution.py:18
  186.9 0.0 collective-permute-start.1
  186.9 0.6 compare_convert_fusion
  187.6 0.8 collective-permute-done.1
  188.4 0.9 add.75
  189.3 1.5 collective-permute-start.2
  190.8 0.1 broadcast_bitcast_fusion
  191.5 2.1 collective-permute-done.2
  193.6 0.4 convolution_multiply_fusion
  194.0 0.9 fusion.19
  194.9 0.0 all-reduce.5.cloned.1.call-update
  194.9 69.3 %all-reduce.5.cloned.1.call-done = f32[4,4096]{1,0:T(4,128)} async-done(((f32[4,4096]{1,0:T(4,128)}), f32[4,4096]{1,0:T(4,128)}) %all-reduce.5.cloned.1.call-update) | async-done | bytes 65552 | tf_op jit(solution)/shard_map/psum | solution.py:18
  264.2 0.0 collective-permute-start.3
  264.2 0.1 dynamic-slice
  264.3 1.4 collective-permute-done.3
  265.7 0.9 add.77
  266.5 1.5 collective-permute-start.4
  268.1 0.6 copy.6
  268.7 2.2 collective-permute-done.4
  270.9 1.9 fusion.18
  272.8 36.1 %psum.38 = f32[4,2048]{1,0:T(4,128)S(1)} all-reduce(f32[4,2048]{1,0:T(4,128)S(1)} %fusion.18), channel_id=1, replica_groups=mesh['leaf'=4,'blk'=8] {'blk'}, use_global_device_ids=true, to_apply=%region_3.0 | all-reduce | flops 8192 | bytes 65536 | tf_op jit(solution)/shard_map/psum | solution.py:18
  308.9 0.0 collective-permute-start.5
  308.9 1.2 collective-permute-done.5
  310.2 2.1 fusion.16
  312.3 33.0 %psum.39 = f32[4,1024]{1,0:T(4,128)S(1)} all-reduce(f32[4,1024]{1,0:T(4,128)S(1)} %fusion.16), channel_id=1, replica_groups=mesh['leaf'=4,'blk'=8] {'blk'}, use_global_device_ids=true, to_apply=%region_4.0 | all-reduce | flops 4096 | bytes 32768 | tf_op jit(solution)/shard_map/psum | solution.py:18
  345.3 0.6 copy.7
  (12 shorter events, 0.2 us)
Async XLA Ops:
  7.2 111.5 %copy-start = (bf16[1,1,128,7168]{3,2,1,0:T(8,128)(2,1)S(1)}, bf16[1,1,128,7168]{3,2,1,0:T(8,128)(2,1)}, u32[]{:S(2)}) copy-start(bf16[1,1,128,7168]{3,2,1,0:T(8,128)(2,1)} %param.5) | copy-start | bytes 5505028
  7.2 179.8 %all-reduce.3.cloned.1.call-start = ((), (), s32[]{:S(2)}) async-start(), calls=%async_computation | async-start | bytes 131072 | tf_op jit(solution)/shard_map/psum | solution.py:18
  117.2 1.4 collective-permute-start
  121.0 143.2 %all-reduce.5.cloned.1.call-start = ((), (), s32[]{:S(2)}) async-start(), calls=%async_computation.1 | async-start | bytes 131072 | tf_op jit(solution)/shard_map/psum | solution.py:18
  186.9 1.5 collective-permute-start.1
  189.3 4.3 %collective-permute-start.2 = (f32[4,4096]{1,0:T(4,128)S(1)}, f32[4,4096]{1,0:T(4,128)S(1)}, u32[]{:S(2)}, u32[]{:S(2)}) collective-permute-start(f32[4,4096]{1,0:T(4,128)S(1)} %add.75), channel_id=1, source_target_pairs={{0,16},{16,0},{8,24},{24,8},{1,17},{17,1},{9,25},{25,9},{2,18},{18... | collective-permute-start | bytes 196616 | tf_op jit(solution)/shard_map/ppermute | solution.py:14
  264.2 1.5 collective-permute-start.3
  266.5 4.3 %collective-permute-start.4 = (f32[4,4096]{1,0:T(4,128)S(1)}, f32[4,4096]{1,0:T(4,128)S(1)}, u32[]{:S(2)}, u32[]{:S(2)}) collective-permute-start(f32[4,4096]{1,0:T(4,128)S(1)} %add.77), channel_id=1, source_target_pairs={{0,16},{16,0},{8,24},{24,8},{1,17},{17,1},{9,25},{25,9},{2,18},{18... | collective-permute-start | bytes 196616 | tf_op jit(solution)/shard_map/ppermute | solution.py:14
  308.9 1.2 collective-permute-start.5
Sparse Core Ops, SparseCore 0:
  121.2 65.7 all-reduce.2
  195.0 69.1 all-reduce.4
where the time goes:
time: 353 us
  blocking collectives  173 us (49%)
  waiting for transfers between devices  143 us (41%)
  between operations  16.1 us (5%)
  matrix products  10.5 us (3%)
  other arithmetic  3.71 us (1%)
    psum x2, waiting for transfers between devices, group_sum(): current = lax.psum(partial_value, 'blk')  135 us
    psum x3, blocking collectives, group_sum(): current = lax.psum(partial_value, 'blk')  102 us
    all_gather x1, blocking collectives, local(): every_side = lax.all_gather(flat_side, ('leaf', 'blk'), axis=1, tiled=True)  71.2 us
    ppermute x6, waiting for transfers between devices, swapped(): return lax.ppermute(block, axis, route)  7.66 us
  transfers between devices with their start and end apart: 8, of which 7 were waited for; matrix products, arithmetic and copies ran while one was open for 1% of the time, Pallas kernels for 0%

commit v1 on v0

v1 whole, which is shorter than its diff:
```python
import jax
import jax.numpy as jnp
from jax import lax
from jax.sharding import PartitionSpec as P

BOTH = ("leaf", "blk")
LAST = (((1,), (1,)), ((), ()))
HALVE_BYTES = 65536


def moved(value, leaf_mask, block_mask):
    leaf_count = lax.axis_size("leaf")
    block_count = lax.axis_size("blk")
    route = []
    for leaf in range(leaf_count):
        for block in range(block_count):
            target = (leaf ^ leaf_mask) * block_count + (block ^ block_mask)
            route.append((leaf * block_count + block, target))
    return lax.ppermute(value, BOTH, route)


def parity():
    index = lax.axis_index("leaf") * lax.axis_size("blk") + lax.axis_index("blk")
    total = index
    for shift in (16, 8, 4, 2, 1):
        total = total ^ (total >> shift)
    return total & 1


def group_sum(value, height):
    block_bits = lax.axis_size("blk").bit_length() - 1
    moves = [(1 << bit | 1, 0) for bit in range(1, height)]
    moves += [(1, 1 << bit) for bit in range(block_bits)]
    if value.size * 4 < HALVE_BYTES:
        value = value + moved(value, 1, 0)
        for move in moves:
            value = value + moved(value, *move)
        return value
    half = value.shape[1] // 2
    odd = parity() == 1
    low, high = value[:, :half], value[:, half:]
    part = jnp.where(odd, high, low) + moved(jnp.where(odd, low, high), 1, 0)
    for move in moves:
        part = part + moved(part, *move)
    other = moved(part, 1, 0)
    return jnp.concatenate([jnp.where(odd, other, part), jnp.where(odd, part, other)], axis=1)


def local(right_side, diag_inverse, update_factor, live_blocks):
    leaf_count = lax.axis_size("leaf")
    block_count = lax.axis_size("blk")
    levels = leaf_count.bit_length()
    leaf_index = lax.axis_index("leaf")
    block_index = lax.axis_index("blk")
    block_rows = diag_inverse.shape[2]
    vectors = right_side.shape[0]
    level_width = block_count * block_rows
    inverse_rows = diag_inverse.reshape(block_rows, -1)
    update_rows = update_factor.reshape(block_rows, -1)
    side = right_side.reshape(vectors, levels * block_rows)
    orders = [(1 << height) * level_width for height in range(levels)]
    spans = [sum(orders[height + 1 :]) for height in range(levels)]
    own_positions, own_masks, group_masks, sides, inverses, updates = [], [], [], [], [], []
    for height in range(levels):
        offset = 2 * leaf_count - (2 * leaf_count >> height)
        live_count = live_blocks[offset + (leaf_index >> height)]
        position = (leaf_index & (1 << height) - 1) * block_count + block_index
        own_positions.append(position)
        own_masks.append((position < live_count).astype(jnp.float32))
        blocks = lax.broadcasted_iota(jnp.int32, (1, orders[height]), 1) // block_rows
        group_masks.append((blocks < live_count).astype(jnp.float32))
        sides.append(side[:, height * block_rows : (height + 1) * block_rows])
        start = ((1 << height) - 1) * level_width
        inverses.append(inverse_rows[:, start : start + orders[height]])
        cursor = sum(spans[:height])
        row = {}
        for ancestor in range(height + 1, levels):
            row[ancestor] = update_rows[:, cursor : cursor + orders[ancestor]]
            cursor += orders[ancestor]
        updates.append(row)

    def own_slot(height):
        blocks = lax.broadcasted_iota(jnp.int32, (1, orders[height]), 1) // block_rows
        tiled = jnp.tile(sides[height], (1, orders[height] // block_rows))
        return jnp.where(blocks == own_positions[height], tiled, 0.0)

    pending = [own_slot(height) for height in range(levels)]
    forward = []
    for height in range(levels):
        if height == 0:
            copies = jnp.broadcast_to(sides[0][None], (block_count, vectors, block_rows))
            source = lax.all_to_all(copies, "blk", 0, 0, tiled=True)
            source = source.transpose(1, 0, 2).reshape(vectors, level_width)
        else:
            source = group_sum(pending[height], height)
        reduced = (group_masks[height] * source).astype(jnp.bfloat16)
        solved = own_masks[height] * lax.dot_general(
            reduced, inverses[height], LAST, preferred_element_type=jnp.float32
        )
        forward.append(solved)
        rounded = solved.astype(jnp.bfloat16)
        for ancestor in range(height + 1, levels):
            pending[ancestor] = pending[ancestor] - jnp.dot(
                rounded, updates[height][ancestor], preferred_element_type=jnp.float32
            )
    residual = list(forward)
    backward = [None] * levels
    for height in reversed(range(levels)):
        weighted = (own_masks[height] * residual[height]).astype(jnp.bfloat16)
        partial = jnp.dot(weighted, inverses[height], preferred_element_type=jnp.float32)
        if height == 0:
            pieces = partial.reshape(vectors, block_count, block_rows).transpose(1, 0, 2)
            backward[0] = own_masks[0] * lax.all_to_all(pieces, "blk", 0, 0, tiled=True).sum(0)
            continue
        whole = group_masks[height] * group_sum(partial, height)
        backward[height] = lax.dynamic_slice_in_dim(
            whole, own_positions[height] * block_rows, block_rows, 1
        )
        rounded = whole.astype(jnp.bfloat16)
        for lower in range(height):
            residual[lower] = residual[lower] - lax.dot_general(
                rounded, updates[lower][height], LAST, preferred_element_type=jnp.float32
            )
    shape = (vectors, 1, 1, levels * block_rows)
    forward_out = jnp.concatenate(forward, axis=1).reshape(shape)
    backward_out = jnp.concatenate(backward, axis=1).reshape(shape)
    return (forward_out, backward_out)


def solution(mesh):
    in_specs = (
        P(None, "leaf", "blk", None),
        P("leaf", "blk", None, None),
        P("leaf", "blk", None, None),
        P(),
    )
    out_specs = (P(None, "leaf", "blk", None), P(None, "leaf", "blk", None))
    return jax.shard_map(local, mesh=mesh, in_specs=in_specs, out_specs=out_specs, check_vma=False)
```

time: 353 us -> 100 us (0.28)
  blocking collectives: 173 us -> 0 us
  waiting for transfers between devices: 143 us -> 60.2 us
  starting transfers between devices: 3.16 us -> 17.3 us
  between operations: 16.1 us -> 2.9 us
    psum x2 -> x0, waiting for transfers between devices: 135 us -> none  [group_sum(): current = lax.psum(partial_value, 'blk')]
    psum x3 -> x0, blocking collectives: 102 us -> none  [group_sum(): current = lax.psum(partial_value, 'blk')]
    all_gather x1 -> x0, blocking collectives: 71.2 us -> none  [local(): every_side = lax.all_gather(flat_side, ('leaf', 'blk'), axis=1, tiled=True)]
    ppermute x6 -> x20, waiting for transfers between devices: 7.66 us -> 49.9 us  [moved(): return lax.ppermute(value, BOTH, route)]
    all_to_all x0 -> x2, starting transfers between devices: none -> 10.6 us  [the longest x1 7.31 us: local(): source = lax.all_to_all(copies, 'blk', 0, 0, tiled=True)]
    all_to_all x0 -> x2, waiting for transfers between devices: none -> 10.3 us  [the longest x1 6.49 us: local(): lax.all_to_all(pieces, 'blk', 0, 0, tiled=True).sum(0)]
    ppermute x6 -> x20, starting transfers between devices: 3.08 us -> 6.64 us  [moved(): return lax.ppermute(value, BOTH, route)]
    dot_general x8 -> x10, matrix products: 10.5 us -> 12.6 us  [the longest x3 5.21 us: local(): jnp.dot(weighted, inverses[height], preferred_element_type=jnp.float32)]
  transfers between devices with their start and end apart: 8 -> 22, of which waited for: 7 -> 21; matrix products, arithmetic and copies ran while one was open for 1% -> 6% of each run, Pallas kernels for 0% -> 0%
where the time goes in v1:
time: 100 us; the launch traced here: 99.3 us
  waiting for transfers between devices  60.2 us (60%)
  starting transfers between devices  17.3 us (17%)
  matrix products  12.6 us (13%)
  local copies, waits for them, and re-layouts  4.11 us (4%)
  between operations  2.9 us (3%)
  other arithmetic  2.29 us (2%)
    ppermute x20, waiting for transfers between devices, moved(): return lax.ppermute(value, BOTH, route)  49.9 us
    all_to_all x1, starting transfers between devices, local(): source = lax.all_to_all(copies, 'blk', 0, 0, tiled=True)  7.31 us
    ppermute x20, starting transfers between devices, moved(): return lax.ppermute(value, BOTH, route)  6.64 us
    all_to_all x1, waiting for transfers between devices, local(): lax.all_to_all(pieces, 'blk', 0, 0, tiled=True).sum(0)  6.49 us
    dot_general x3, matrix products, local(): jnp.dot(weighted, inverses[height], preferred_element_type=jnp.float32)  5.21 us
    dot_general x3, matrix products, local(): lax.dot_general(reduced, inverses[height], LAST, preferred_element_type=j...  3.99 us
    all_to_all x1, waiting for transfers between devices, local(): source = lax.all_to_all(copies, 'blk', 0, 0, tiled=True)  3.82 us
    all_to_all x1, starting transfers between devices, local(): lax.all_to_all(pieces, 'blk', 0, 0, tiled=True).sum(0)  3.32 us
  transfers between devices with their start and end apart: 22, of which 21 were waited for; matrix products, arithmetic and copies ran while one was open for 6% of the time, Pallas kernels for 0%

profile of v1, /device:TPU:0, one launch (start us, length us, event | category | flops | bytes accessed | tf_op | source)
XLA Modules:
  0.0 99.3 jit_solution(7353575343868956149)
XLA Ops:
  0.6 0.0 copy-start
  0.6 0.8 copy.17
  1.5 0.6 broadcast_in_dim.30
  2.1 7.3 %all-to-all-start = ((f32[8,4,128]{2,1,0:T(4,128)}), f32[8,4,128]{2,1,0:T(4,128)S(1)}, u32[]{:S(2)}, u32[]{:S(2)}) async-start(f32[8,4,128]{2,1,0:T(4,128)} %broadcast_in_dim.30), calls=%async_computation | async-start | bytes 32768 | tf_op jit(solution)/shard_map/all_to_all | solution.py:92
  9.4 1.4 %fusion.57 = (s32[1]{0:T(128)}, s32[1]{0:T(128)}, s32[1]{0:T(128)}) fusion(s32[7]{0:T(128)} %param.7, s32[]{:T(128)S(6)} %select_n.106, s32[]{:T(128)S(6)} %select_n.101, s32[]{:T(128)S(6)} %select_n.103), kind=kLoop, calls=%fused_computation.97 | loop fusion | bytes 36 | tf_op jit(solution)/shard_map/dynamic_slice | solution.py:66
  10.8 0.6 fusion.48
  12.2 3.8 %all-to-all-done = f32[8,4,128]{2,1,0:T(4,128)S(1)} async-done(((f32[8,4,128]{2,1,0:T(4,128)}), f32[8,4,128]{2,1,0:T(4,128)S(1)}, u32[]{:S(2)}, u32[]{:S(2)}) %all-to-all-start) | async-done | bytes 16416 | tf_op jit(solution)/shard_map/all_to_all | solution.py:92
  16.0 1.1 %convolution_multiply_fusion.1 = f32[4,128]{1,0:T(4,128)S(1)} fusion(bf16[128,7168]{1,0:T(8,128)(2,1)} %bitcast.41, f32[8,4,128]{2,1,0:T(4,128)S(1)} %all-to-all-done, f32[1024]{0:T(1024)S(1)} %fusion.48, f32[]{:T(128)S(6)} %convert_element_type.63), kind=kOutput, calls=%fused_computation.8 | convolution fusion | flops 1057280 | bytes 284676 | tf_op jit(solution)/shard_map/dot_general | solution.py:97
  17.1 1.2 %convolution_subtract_fusion.2 = f32[4,2048]{1,0:T(4,128)S(1)} fusion(bf16[128,10240]{1,0:T(8,128)(2,1)} %bitcast.35, f32[1,4,16,128]{3,2,1,0:T(8,128)S(1)} %broadcast_bitcast_fusion.1, pred[2048]{0:T(1024)(128)(4,1)S(1)} %fusion.38, f32[4,128]{1,0:T(4,128)S(1)} %convolution_multiply_fusion.1), kind=kOutput, calls=%fused_computation.2 | convolution fusion | flops 2114048 | bytes 593920 | tf_op jit(solution)/shard_map/dot_general | solution.py:103
  18.3 0.0 collective-permute-start
  18.4 1.2 %collective-permute-done = f32[4,2048]{1,0:T(4,128)S(1)} collective-permute-done((f32[4,2048]{1,0:T(4,128)S(1)}, f32[4,2048]{1,0:T(4,128)S(1)}, u32[]{:S(2)}, u32[]{:S(2)}) %collective-permute-start) | collective-permute-done | bytes 32800 | tf_op jit(solution)/shard_map/ppermute | solution.py:19
  19.6 0.4 collective-permute-start.1
  20.0 0.7 fusion.42
  20.6 2.4 %collective-permute-done.1 = f32[4,2048]{1,0:T(4,128)S(1)} collective-permute-done((f32[4,2048]{1,0:T(4,128)S(1)}, f32[4,2048]{1,0:T(4,128)S(1)}, u32[]{:S(2)}, u32[]{:S(2)}) %collective-permute-start.1) | collective-permute-done | bytes 32800 | tf_op jit(solution)/shard_map/ppermute | solution.py:19
  23.0 0.3 collective-permute-start.2
  24.0 2.4 %collective-permute-done.2 = f32[4,2048]{1,0:T(4,128)S(1)} collective-permute-done((f32[4,2048]{1,0:T(4,128)S(1)}, f32[4,2048]{1,0:T(4,128)S(1)}, u32[]{:S(2)}, u32[]{:S(2)}) %collective-permute-start.2) | collective-permute-done | bytes 32800 | tf_op jit(solution)/shard_map/ppermute | solution.py:19
  26.4 0.4 collective-permute-start.3
  26.8 1.5 %convolution_subtract_fusion.1 = f32[4,4096]{1,0:T(4,128)S(1)} fusion(bf16[128,10240]{1,0:T(8,128)(2,1)} %bitcast.36, f32[1,4,32,128]{3,2,1,0:T(8,128)S(1)} %broadcast_bitcast_fusion, pred[4096]{0:T(1024)(128)(4,1)S(1)} %fusion.25, f32[4,128]{1,0:T(4,128)S(1)} %convolution_multiply_fusion.1), kind=kOutput, calls=%fused_computation.1 | convolution fusion | flops 4227584 | bytes 1185792 | tf_op jit(solution)/shard_map/dot_general | solution.py:103
  28.3 3.4 %collective-permute-done.3 = f32[4,2048]{1,0:T(4,128)S(1)} collective-permute-done((f32[4,2048]{1,0:T(4,128)S(1)}, f32[4,2048]{1,0:T(4,128)S(1)}, u32[]{:S(2)}, u32[]{:S(2)}) %collective-permute-start.3) | collective-permute-done | bytes 32800 | tf_op jit(solution)/shard_map/ppermute | solution.py:19
  31.7 1.3 %convolution_multiply_fusion.2 = f32[4,128]{1,0:T(4,128)S(1)} fusion(bf16[128,7168]{1,0:T(8,128)(2,1)} %bitcast.42, f32[4,2048]{1,0:T(4,128)S(1)} %add.116, f32[4,2048]{1,0:T(4,128)S(1)} %collective-permute-done.3, f32[2048]{0:T(1024)S(1)} %fusion.42, f32[]{:T(128)S(6)} %convert_element_type.66), kind=kOutput, calls=%fused_computation.11 | convolution fusion | flops 2122240 | bytes 600068 | tf_op jit(solution)/shard_map/dot_general | solution.py:97
  33.0 0.0 copy-done
  33.0 0.3 convolution_subtract_fusion
  33.3 0.2 collective-permute-start.4
  33.4 1.1 %collective-permute-done.4 = f32[4,2048]{1,0:T(4,128)S(1)} collective-permute-done((f32[4,2048]{1,0:T(4,128)S(1)}, f32[4,2048]{1,0:T(4,128)S(1)}, u32[]{:S(2)}, u32[]{:S(2)}) %collective-permute-start.4) | collective-permute-done | bytes 32800 | tf_op jit(solution)/shard_map/ppermute | solution.py:19
  34.5 1.3 %collective-permute-start.5 = (f32[4,2048]{1,0:T(4,128)S(1)}, f32[4,2048]{1,0:T(4,128)S(1)}, u32[]{:S(2)}, u32[]{:S(2)}) collective-permute-start(f32[4,2048]{1,0:T(4,128)S(1)} %select_add_fusion.1), channel_id=1, source_target_pairs={{0,24},{1,25},{2,26},{3,27},{4,28},{5,29},{6,30},{7,31},{8,16},{9,... | collective-permute-start | bytes 98312 | tf_op jit(solution)/shard_map/ppermute | solution.py:19
  35.9 2.1 %collective-permute-done.5 = f32[4,2048]{1,0:T(4,128)S(1)} collective-permute-done((f32[4,2048]{1,0:T(4,128)S(1)}, f32[4,2048]{1,0:T(4,128)S(1)}, u32[]{:S(2)}, u32[]{:S(2)}) %collective-permute-start.5) | collective-permute-done | bytes 32800 | tf_op jit(solution)/shard_map/ppermute | solution.py:19
  38.0 0.3 collective-permute-start.6
  38.3 3.1 %collective-permute-done.6 = f32[4,2048]{1,0:T(4,128)S(1)} collective-permute-done((f32[4,2048]{1,0:T(4,128)S(1)}, f32[4,2048]{1,0:T(4,128)S(1)}, u32[]{:S(2)}, u32[]{:S(2)}) %collective-permute-start.6) | collective-permute-done | bytes 32800 | tf_op jit(solution)/shard_map/ppermute | solution.py:19
  41.4 0.1 collective-permute-start.7
  41.5 3.3 %collective-permute-done.7 = f32[4,2048]{1,0:T(4,128)S(1)} collective-permute-done((f32[4,2048]{1,0:T(4,128)S(1)}, f32[4,2048]{1,0:T(4,128)S(1)}, u32[]{:S(2)}, u32[]{:S(2)}) %collective-permute-start.7) | collective-permute-done | bytes 32800 | tf_op jit(solution)/shard_map/ppermute | solution.py:19
  44.8 0.1 collective-permute-start.8
  44.9 4.8 %collective-permute-done.8 = f32[4,2048]{1,0:T(4,128)S(1)} collective-permute-done((f32[4,2048]{1,0:T(4,128)S(1)}, f32[4,2048]{1,0:T(4,128)S(1)}, u32[]{:S(2)}, u32[]{:S(2)}) %collective-permute-start.8) | collective-permute-done | bytes 32800 | tf_op jit(solution)/shard_map/ppermute | solution.py:19
  49.7 0.2 collective-permute-start.9
  49.9 0.6 fusion.34
  51.2 0.0 collective-permute-done.9
  51.2 1.6 %convolution_multiply_fusion = f32[4,128]{1,0:T(4,128)S(1)} fusion(bf16[128,7168]{1,0:T(8,128)(2,1)} %bitcast.43, f32[4,2048]{1,0:T(4,128)S(1)} %get-tuple-element.9, f32[4,2048]{1,0:T(4,128)S(1)} %get-tuple-element.8, f32[4096]{0:T(1024)S(1)} %fusion.34, f32[]{:T(128)S(6)} %convert_element_type.70), kind=kOutput, calls=%fused_computation.7 | convolution fusion | flops 4243968 | bytes 1132548 | tf_op jit(solution)/shard_map/dot_general | solution.py:97
  52.8 1.5 %fusion.5 = f32[4,4096]{1,0:T(4,128)S(1)} fusion(bf16[128,7168]{1,0:T(8,128)(2,1)} %bitcast.44, f32[4,128]{1,0:T(4,128)S(1)} %convolution_multiply_fusion, f32[]{:T(128)S(6)} %convert_element_type.70), kind=kOutput, calls=%fused_computation.15 | convolution fusion | flops 4195328 | bytes 1116164 | tf_op jit(solution)/shard_map/dot_general | solution.py:110
  54.3 0.5 collective-permute-start.10
  54.8 0.9 collective-permute-done.10
  55.7 1.5 %collective-permute-start.11 = (f32[4,2048]{1,0:T(4,128)S(1)}, f32[4,2048]{1,0:T(4,128)S(1)}, u32[]{:S(2)}, u32[]{:S(2)}) collective-permute-start(f32[4,2048]{1,0:T(4,128)S(1)} %select_add_fusion), channel_id=1, source_target_pairs={{0,24},{1,25},{2,26},{3,27},{4,28},{5,29},{6,30},{7,31},{8,16},{9,... | collective-permute-start | bytes 98312 | tf_op jit(solution)/shard_map/ppermute | solution.py:19
  57.2 1.9 %collective-permute-done.11 = f32[4,2048]{1,0:T(4,128)S(1)} collective-permute-done((f32[4,2048]{1,0:T(4,128)S(1)}, f32[4,2048]{1,0:T(4,128)S(1)}, u32[]{:S(2)}, u32[]{:S(2)}) %collective-permute-start.11) | collective-permute-done | bytes 32800 | tf_op jit(solution)/shard_map/ppermute | solution.py:19
  59.1 0.5 collective-permute-start.12
  59.6 2.9 %collective-permute-done.12 = f32[4,2048]{1,0:T(4,128)S(1)} collective-permute-done((f32[4,2048]{1,0:T(4,128)S(1)}, f32[4,2048]{1,0:T(4,128)S(1)}, u32[]{:S(2)}, u32[]{:S(2)}) %collective-permute-start.12) | collective-permute-done | bytes 32800 | tf_op jit(solution)/shard_map/ppermute | solution.py:19
  62.5 0.1 collective-permute-start.13
  62.6 3.3 %collective-permute-done.13 = f32[4,2048]{1,0:T(4,128)S(1)} collective-permute-done((f32[4,2048]{1,0:T(4,128)S(1)}, f32[4,2048]{1,0:T(4,128)S(1)}, u32[]{:S(2)}, u32[]{:S(2)}) %collective-permute-start.13) | collective-permute-done | bytes 32800 | tf_op jit(solution)/shard_map/ppermute | solution.py:19
  65.9 0.1 collective-permute-start.14
  66.0 4.8 %collective-permute-done.14 = f32[4,2048]{1,0:T(4,128)S(1)} collective-permute-done((f32[4,2048]{1,0:T(4,128)S(1)}, f32[4,2048]{1,0:T(4,128)S(1)}, u32[]{:S(2)}, u32[]{:S(2)}) %collective-permute-start.14) | collective-permute-done | bytes 32800 | tf_op jit(solution)/shard_map/ppermute | solution.py:19
  70.8 0.2 collective-permute-start.15
  71.0 1.1 %collective-permute-done.15 = f32[4,2048]{1,0:T(4,128)S(1)} collective-permute-done((f32[4,2048]{1,0:T(4,128)S(1)}, f32[4,2048]{1,0:T(4,128)S(1)}, u32[]{:S(2)}, u32[]{:S(2)}) %collective-permute-start.15) | collective-permute-done | bytes 32800 | tf_op jit(solution)/shard_map/ppermute | solution.py:19
  72.2 1.7 %fusion.4 = f32[4,2048]{1,0:T(4,128)S(1)} fusion(f32[4,128]{1,0:T(4,128)S(1)} %convolution_multiply_fusion.2, bf16[128,10240]{1,0:T(8,128)(2,1)S(1)} %bitcast.38, bf16[128,7168]{1,0:T(8,128)(2,1)} %bitcast.45, f32[4,4096]{1,0:T(4,128)S(1)} %maximum_multiply_fusion.1, f32[]{:T(128)S(6)} %convert_element_type.66), kind=kOutput, calls=%fused_computation.14 | convolution fusion | flops 6309376 | bytes 1673220 | tf_op jit(solution)/shard_map/dot_general | solution.py:110
  73.9 0.2 collective-permute-start.16
  74.1 1.0 %collective-permute-done.16 = f32[4,2048]{1,0:T(4,128)S(1)} collective-permute-done((f32[4,2048]{1,0:T(4,128)S(1)}, f32[4,2048]{1,0:T(4,128)S(1)}, u32[]{:S(2)}, u32[]{:S(2)}) %collective-permute-start.16) | collective-permute-done | bytes 32800 | tf_op jit(solution)/shard_map/ppermute | solution.py:19
  75.1 0.3 collective-permute-start.17
  75.4 0.6 copy.9
  76.0 2.5 %collective-permute-done.17 = f32[4,2048]{1,0:T(4,128)S(1)} collective-permute-done((f32[4,2048]{1,0:T(4,128)S(1)}, f32[4,2048]{1,0:T(4,128)S(1)}, u32[]{:S(2)}, u32[]{:S(2)}) %collective-permute-start.17) | collective-permute-done | bytes 32800 | tf_op jit(solution)/shard_map/ppermute | solution.py:19
  78.5 0.1 collective-permute-start.18
  78.6 0.4 convolution_subtract_fusion.4
  79.0 3.0 %collective-permute-done.18 = f32[4,2048]{1,0:T(4,128)S(1)} collective-permute-done((f32[4,2048]{1,0:T(4,128)S(1)}, f32[4,2048]{1,0:T(4,128)S(1)}, u32[]{:S(2)}, u32[]{:S(2)}) %collective-permute-start.18) | collective-permute-done | bytes 32800 | tf_op jit(solution)/shard_map/ppermute | solution.py:19
  82.0 0.1 collective-permute-start.19
  82.1 4.8 %collective-permute-done.19 = f32[4,2048]{1,0:T(4,128)S(1)} collective-permute-done((f32[4,2048]{1,0:T(4,128)S(1)}, f32[4,2048]{1,0:T(4,128)S(1)}, u32[]{:S(2)}, u32[]{:S(2)}) %collective-permute-start.19) | collective-permute-done | bytes 32800 | tf_op jit(solution)/shard_map/ppermute | solution.py:19
  86.9 2.0 %convolution_bitcast_fusion = f32[8,4,128]{2,1,0:T(4,128)} fusion(f32[4,128]{1,0:T(4,128)S(1)} %convolution_subtract_fusion.4, bf16[128,10240]{1,0:T(8,128)(2,1)S(1)} %bitcast.40, bf16[128,7168]{1,0:T(8,128)(2,1)} %bitcast.46, f32[4,2048]{1,0:T(4,128)S(1)} %add_multiply_fusion, f32[]{:T(128)S(6)} %convert_element_type.63), kind=kOutput, calls=%fused_computation.3 | convolution fusion | flops 3155456 | bytes 837636 | tf_op jit(solution)/shard_map/dot_general | solution.py:110
  88.9 3.3 %all-to-all-start.1 = ((f32[8,4,128]{2,1,0:T(4,128)}), f32[8,4,128]{2,1,0:T(4,128)S(1)}, u32[]{:S(2)}, u32[]{:S(2)}) async-start(f32[8,4,128]{2,1,0:T(4,128)} %convolution_bitcast_fusion), calls=%async_computation.1 | async-start | bytes 32768 | tf_op jit(solution)/shard_map/all_to_all | solution.py:113
  92.2 6.5 %all-to-all-done.1 = f32[8,4,128]{2,1,0:T(4,128)S(1)} async-done(((f32[8,4,128]{2,1,0:T(4,128)}), f32[8,4,128]{2,1,0:T(4,128)S(1)}, u32[]{:S(2)}, u32[]{:S(2)}) %all-to-all-start.1) | async-done | bytes 16416 | tf_op jit(solution)/shard_map/all_to_all | solution.py:113
  98.7 0.6 copy.10
  (33 shorter events, 0.4 us)
Async XLA Ops:
  0.6 32.3 %copy-start = (bf16[1,1,128,10240]{3,2,1,0:T(8,128)(2,1)S(1)}, bf16[1,1,128,10240]{3,2,1,0:T(8,128)(2,1)}, u32[]{:S(2)}) copy-start(bf16[1,1,128,10240]{3,2,1,0:T(8,128)(2,1)} %param.6) | copy-start | bytes 7864324
  2.1 13.9 %all-to-all-start = ((f32[8,4,128]{2,1,0:T(4,128)}), f32[8,4,128]{2,1,0:T(4,128)S(1)}, u32[]{:S(2)}, u32[]{:S(2)}) async-start(f32[8,4,128]{2,1,0:T(4,128)} %broadcast_in_dim.30), calls=%async_computation | async-start | bytes 32768 | tf_op jit(solution)/shard_map/all_to_all | solution.py:92
  18.3 1.2 %collective-permute-start = (f32[4,2048]{1,0:T(4,128)S(1)}, f32[4,2048]{1,0:T(4,128)S(1)}, u32[]{:S(2)}, u32[]{:S(2)}) collective-permute-start(f32[4,2048]{1,0:T(4,128)S(1)} %convolution_subtract_fusion.2), channel_id=1, source_target_pairs={{0,8},{1,9},{2,10},{3,11},{4,12},{5,13},{6,14},{7,15},{8,0},{9,1},... | collective-permute-start | bytes 98312 | tf_op jit(solution)/shard_map/ppermute | solution.py:19
  19.6 3.4 %collective-permute-start.1 = (f32[4,2048]{1,0:T(4,128)S(1)}, f32[4,2048]{1,0:T(4,128)S(1)}, u32[]{:S(2)}, u32[]{:S(2)}) collective-permute-start(f32[4,2048]{1,0:T(4,128)S(1)} %add.114), channel_id=1, source_target_pairs={{0,9},{1,8},{2,11},{3,10},{4,13},{5,12},{6,15},{7,14},{8,1},{9,0},... | collective-permute-start | bytes 98312 | tf_op jit(solution)/shard_map/ppermute | solution.py:19
  23.0 3.4 %collective-permute-start.2 = (f32[4,2048]{1,0:T(4,128)S(1)}, f32[4,2048]{1,0:T(4,128)S(1)}, u32[]{:S(2)}, u32[]{:S(2)}) collective-permute-start(f32[4,2048]{1,0:T(4,128)S(1)} %add.115), channel_id=1, source_target_pairs={{0,10},{1,11},{2,8},{3,9},{4,14},{5,15},{6,12},{7,13},{8,2},{9,3},... | collective-permute-start | bytes 98312 | tf_op jit(solution)/shard_map/ppermute | solution.py:19
  26.4 5.2 %collective-permute-start.3 = (f32[4,2048]{1,0:T(4,128)S(1)}, f32[4,2048]{1,0:T(4,128)S(1)}, u32[]{:S(2)}, u32[]{:S(2)}) collective-permute-start(f32[4,2048]{1,0:T(4,128)S(1)} %add.116), channel_id=1, source_target_pairs={{0,12},{1,13},{2,14},{3,15},{4,8},{5,9},{6,10},{7,11},{8,4},{9,5},... | collective-permute-start | bytes 98312 | tf_op jit(solution)/shard_map/ppermute | solution.py:19
  33.3 1.3 %collective-permute-start.4 = (f32[4,2048]{1,0:T(4,128)S(1)}, f32[4,2048]{1,0:T(4,128)S(1)}, u32[]{:S(2)}, u32[]{:S(2)}) collective-permute-start(f32[4,2048]{1,0:T(4,128)S(1)} %slice_select_fusion.1), channel_id=1, source_target_pairs={{0,8},{1,9},{2,10},{3,11},{4,12},{5,13},{6,14},{7,15},{8,0},{9,1},... | collective-permute-start | bytes 98312 | tf_op jit(solution)/shard_map/ppermute | solution.py:19
  34.5 3.4 %collective-permute-start.5 = (f32[4,2048]{1,0:T(4,128)S(1)}, f32[4,2048]{1,0:T(4,128)S(1)}, u32[]{:S(2)}, u32[]{:S(2)}) collective-permute-start(f32[4,2048]{1,0:T(4,128)S(1)} %select_add_fusion.1), channel_id=1, source_target_pairs={{0,24},{1,25},{2,26},{3,27},{4,28},{5,29},{6,30},{7,31},{8,16},{9,... | collective-permute-start | bytes 98312 | tf_op jit(solution)/shard_map/ppermute | solution.py:19
  38.0 3.4 %collective-permute-start.6 = (f32[4,2048]{1,0:T(4,128)S(1)}, f32[4,2048]{1,0:T(4,128)S(1)}, u32[]{:S(2)}, u32[]{:S(2)}) collective-permute-start(f32[4,2048]{1,0:T(4,128)S(1)} %add.122), channel_id=1, source_target_pairs={{0,9},{1,8},{2,11},{3,10},{4,13},{5,12},{6,15},{7,14},{8,1},{9,0},... | collective-permute-start | bytes 98312 | tf_op jit(solution)/shard_map/ppermute | solution.py:19
  41.4 3.4 %collective-permute-start.7 = (f32[4,2048]{1,0:T(4,128)S(1)}, f32[4,2048]{1,0:T(4,128)S(1)}, u32[]{:S(2)}, u32[]{:S(2)}) collective-permute-start(f32[4,2048]{1,0:T(4,128)S(1)} %add.123), channel_id=1, source_target_pairs={{0,10},{1,11},{2,8},{3,9},{4,14},{5,15},{6,12},{7,13},{8,2},{9,3},... | collective-permute-start | bytes 98312 | tf_op jit(solution)/shard_map/ppermute | solution.py:19
  44.8 4.9 %collective-permute-start.8 = (f32[4,2048]{1,0:T(4,128)S(1)}, f32[4,2048]{1,0:T(4,128)S(1)}, u32[]{:S(2)}, u32[]{:S(2)}) collective-permute-start(f32[4,2048]{1,0:T(4,128)S(1)} %add.124), channel_id=1, source_target_pairs={{0,12},{1,13},{2,14},{3,15},{4,8},{5,9},{6,10},{7,11},{8,4},{9,5},... | collective-permute-start | bytes 98312 | tf_op jit(solution)/shard_map/ppermute | solution.py:19
  49.7 1.5 %collective-permute-start.9 = (f32[4,2048]{1,0:T(4,128)S(1)}, f32[4,2048]{1,0:T(4,128)S(1)}, u32[]{:S(2)}, u32[]{:S(2)}) collective-permute-start(f32[4,2048]{1,0:T(4,128)S(1)} %add.125), channel_id=1, source_target_pairs={{0,8},{1,9},{2,10},{3,11},{4,12},{5,13},{6,14},{7,15},{8,0},{9,1},... | collective-permute-start | bytes 98312 | tf_op jit(solution)/shard_map/ppermute | solution.py:19
  54.3 1.3 %collective-permute-start.10 = (f32[4,2048]{1,0:T(4,128)S(1)}, f32[4,2048]{1,0:T(4,128)S(1)}, u32[]{:S(2)}, u32[]{:S(2)}) collective-permute-start(f32[4,2048]{1,0:T(4,128)S(1)} %slice_select_fusion), channel_id=1, source_target_pairs={{0,8},{1,9},{2,10},{3,11},{4,12},{5,13},{6,14},{7,15},{8,0},{9,1},... | collective-permute-start | bytes 98312 | tf_op jit(solution)/shard_map/ppermute | solution.py:19
  55.7 3.4 %collective-permute-start.11 = (f32[4,2048]{1,0:T(4,128)S(1)}, f32[4,2048]{1,0:T(4,128)S(1)}, u32[]{:S(2)}, u32[]{:S(2)}) collective-permute-start(f32[4,2048]{1,0:T(4,128)S(1)} %select_add_fusion), channel_id=1, source_target_pairs={{0,24},{1,25},{2,26},{3,27},{4,28},{5,29},{6,30},{7,31},{8,16},{9,... | collective-permute-start | bytes 98312 | tf_op jit(solution)/shard_map/ppermute | solution.py:19
  59.1 3.4 %collective-permute-start.12 = (f32[4,2048]{1,0:T(4,128)S(1)}, f32[4,2048]{1,0:T(4,128)S(1)}, u32[]{:S(2)}, u32[]{:S(2)}) collective-permute-start(f32[4,2048]{1,0:T(4,128)S(1)} %add.127), channel_id=1, source_target_pairs={{0,9},{1,8},{2,11},{3,10},{4,13},{5,12},{6,15},{7,14},{8,1},{9,0},... | collective-permute-start | bytes 98312 | tf_op jit(solution)/shard_map/ppermute | solution.py:19
  62.5 3.4 %collective-permute-start.13 = (f32[4,2048]{1,0:T(4,128)S(1)}, f32[4,2048]{1,0:T(4,128)S(1)}, u32[]{:S(2)}, u32[]{:S(2)}) collective-permute-start(f32[4,2048]{1,0:T(4,128)S(1)} %add.128), channel_id=1, source_target_pairs={{0,10},{1,11},{2,8},{3,9},{4,14},{5,15},{6,12},{7,13},{8,2},{9,3},... | collective-permute-start | bytes 98312 | tf_op jit(solution)/shard_map/ppermute | solution.py:19
  65.9 4.9 %collective-permute-start.14 = (f32[4,2048]{1,0:T(4,128)S(1)}, f32[4,2048]{1,0:T(4,128)S(1)}, u32[]{:S(2)}, u32[]{:S(2)}) collective-permute-start(f32[4,2048]{1,0:T(4,128)S(1)} %add.129), channel_id=1, source_target_pairs={{0,12},{1,13},{2,14},{3,15},{4,8},{5,9},{6,10},{7,11},{8,4},{9,5},... | collective-permute-start | bytes 98312 | tf_op jit(solution)/shard_map/ppermute | solution.py:19
  70.8 1.3 %collective-permute-start.15 = (f32[4,2048]{1,0:T(4,128)S(1)}, f32[4,2048]{1,0:T(4,128)S(1)}, u32[]{:S(2)}, u32[]{:S(2)}) collective-permute-start(f32[4,2048]{1,0:T(4,128)S(1)} %add.130), channel_id=1, source_target_pairs={{0,8},{1,9},{2,10},{3,11},{4,12},{5,13},{6,14},{7,15},{8,0},{9,1},... | collective-permute-start | bytes 98312 | tf_op jit(solution)/shard_map/ppermute | solution.py:19
  73.9 1.2 %collective-permute-start.16 = (f32[4,2048]{1,0:T(4,128)S(1)}, f32[4,2048]{1,0:T(4,128)S(1)}, u32[]{:S(2)}, u32[]{:S(2)}) collective-permute-start(f32[4,2048]{1,0:T(4,128)S(1)} %fusion.4), channel_id=1, source_target_pairs={{0,8},{1,9},{2,10},{3,11},{4,12},{5,13},{6,14},{7,15},{8,0},{9,1},... | collective-permute-start | bytes 98312 | tf_op jit(solution)/shard_map/ppermute | solution.py:19
  75.1 3.4 %collective-permute-start.17 = (f32[4,2048]{1,0:T(4,128)S(1)}, f32[4,2048]{1,0:T(4,128)S(1)}, u32[]{:S(2)}, u32[]{:S(2)}) collective-permute-start(f32[4,2048]{1,0:T(4,128)S(1)} %add.131), channel_id=1, source_target_pairs={{0,9},{1,8},{2,11},{3,10},{4,13},{5,12},{6,15},{7,14},{8,1},{9,0},... | collective-permute-start | bytes 98312 | tf_op jit(solution)/shard_map/ppermute | solution.py:19
  78.5 3.4 %collective-permute-start.18 = (f32[4,2048]{1,0:T(4,128)S(1)}, f32[4,2048]{1,0:T(4,128)S(1)}, u32[]{:S(2)}, u32[]{:S(2)}) collective-permute-start(f32[4,2048]{1,0:T(4,128)S(1)} %add.132), channel_id=1, source_target_pairs={{0,10},{1,11},{2,8},{3,9},{4,14},{5,15},{6,12},{7,13},{8,2},{9,3},... | collective-permute-start | bytes 98312 | tf_op jit(solution)/shard_map/ppermute | solution.py:19
  82.0 4.9 %collective-permute-start.19 = (f32[4,2048]{1,0:T(4,128)S(1)}, f32[4,2048]{1,0:T(4,128)S(1)}, u32[]{:S(2)}, u32[]{:S(2)}) collective-permute-start(f32[4,2048]{1,0:T(4,128)S(1)} %add.133), channel_id=1, source_target_pairs={{0,12},{1,13},{2,14},{3,15},{4,8},{5,9},{6,10},{7,11},{8,4},{9,5},... | collective-permute-start | bytes 98312 | tf_op jit(solution)/shard_map/ppermute | solution.py:19
  88.9 9.8 %all-to-all-start.1 = ((f32[8,4,128]{2,1,0:T(4,128)}), f32[8,4,128]{2,1,0:T(4,128)S(1)}, u32[]{:S(2)}, u32[]{:S(2)}) async-start(f32[8,4,128]{2,1,0:T(4,128)} %convolution_bitcast_fusion), calls=%async_computation.1 | async-start | bytes 32768 | tf_op jit(solution)/shard_map/all_to_all | solution.py:113

commit v2 on v1

v2 whole, which is shorter than its diff:
```python
import functools

import jax
import jax.numpy as jnp
from jax import lax
from jax.experimental import pallas as pl
from jax.experimental.pallas import tpu as pltpu
from jax.sharding import PartitionSpec as P

BOTH = ("leaf", "blk")
LAST = (((1,), (1,)), ((), ()))
HALVE_BYTES = 65536
VMEM_LIMIT = 8 << 20
F32 = jnp.float32
BF16 = jnp.bfloat16


def moved(value, leaf_mask, block_mask):
    leaf_count = lax.axis_size("leaf")
    block_count = lax.axis_size("blk")
    route = []
    for leaf in range(leaf_count):
        for block in range(block_count):
            target = (leaf ^ leaf_mask) * block_count + (block ^ block_mask)
            route.append((leaf * block_count + block, target))
    return lax.ppermute(value, BOTH, route)


def group_moves(height):
    block_bits = lax.axis_size("blk").bit_length() - 1
    return [(1 << bit | 1, 0) for bit in range(1, height)] + [(1, 1 << bit) for bit in range(block_bits)]


def group_sum(values, height):
    if len(values) == 1:
        value = values[0] + moved(values[0], 1, 0)
        for move in group_moves(height):
            value = value + moved(value, *move)
        return (value,)
    part = values[0] + moved(values[1], 1, 0)
    for move in group_moves(height):
        part = part + moved(part, *move)
    return part, moved(part, 1, 0)


class Plan:
    def __init__(self, vectors, block_rows):
        self.leaf_count = lax.axis_size("leaf")
        self.block_count = lax.axis_size("blk")
        self.levels = self.leaf_count.bit_length()
        self.vectors = vectors
        self.rows = block_rows
        self.orders = [(1 << h) * self.block_count * block_rows for h in range(self.levels)]

    def halved(self, height):
        return height > 0 and self.orders[height] * self.vectors * 4 >= HALVE_BYTES

    def position(self, height):
        leaf = lax.axis_index("leaf") & (1 << height) - 1
        return leaf * self.block_count + lax.axis_index("blk")

    def odd(self):
        total = lax.axis_index("leaf") * self.block_count + lax.axis_index("blk")
        for shift in (16, 8, 4, 2, 1):
            total = total ^ (total >> shift)
        return total & 1

    def own_mask(self, lives_ref, height):
        return (self.position(height) < lives_ref[height]).astype(F32)

    def blocks(self, array):
        return [array[:, i : i + self.rows] for i in range(0, array.shape[1], self.rows)]

    def slotted(self, side, height, start, values):
        first = self.position(height) - start // self.rows
        ids = lax.broadcasted_iota(jnp.int32, side.shape, 1) * 0 + first
        parts = [jnp.where(ids == j, value + side, value) for j, value in enumerate(self.blocks(values))]
        return jnp.concatenate(parts, axis=1)

    def masked(self, lives_ref, height, source):
        if len(source) == 2:
            odd = jnp.full((self.vectors, self.rows), self.odd(), jnp.int32) == 1
            parts, others = self.blocks(source[0][...]), self.blocks(source[1][...])
            found = [jnp.where(odd, b, a) for a, b in zip(parts, others)]
            found += [jnp.where(odd, a, b) for a, b in zip(parts, others)]
        elif len(source[0].shape) == 3:
            found = [source[0][j] for j in range(self.block_count)]
        else:
            found = self.blocks(source[0][...])
        lives = lives_ref[height]
        return [jnp.where(lives > j, value, 0.0) for j, value in enumerate(found)]

    def spread_out(self, height):
        width = self.orders[height]
        if self.halved(height):
            return [(self.vectors, width // 2)] * 2
        return [(self.vectors, width)]

    def ranges(self, height):
        width = self.orders[height]
        if not self.halved(height):
            return [(0, width)]
        half = width // 2
        odd = self.odd()
        return [(pl.multiple_of(odd * half, half), half), (pl.multiple_of((1 - odd) * half, half), half)]


def call(body, name, outs, arguments):
    return pl.pallas_call(
        body,
        in_specs=[pl.BlockSpec(memory_space=pltpu.VMEM)] * len(arguments),
        out_specs=[pl.BlockSpec(memory_space=pltpu.VMEM)] * len(outs),
        out_shape=[pltpu.VMEM(shape, kind) for shape, kind in outs],
        compiler_params=pltpu.CompilerParams(vmem_limit_bytes=VMEM_LIMIT),
        name=name,
    )(*arguments)


def resident(inverse_rows, update_rows, inverse_cuts, update_cuts):
    cuts = [(0, *cut) for cut in inverse_cuts] + [(1, *cut) for cut in update_cuts]
    rows = inverse_rows.shape[2]

    def kernel(inverse_ref, update_ref, *rest):
        outs, sems = rest[: len(cuts)], rest[len(cuts)]
        copies = []
        for index, (which, start, width) in enumerate(cuts):
            source = (inverse_ref, update_ref)[which].at[0, 0, :, pl.ds(start, width)]
            copies.append(pltpu.make_async_copy(source, outs[index], sems.at[index]))
        for copy in copies:
            copy.start()
        for copy in copies:
            copy.wait()

    return pl.pallas_call(
        kernel,
        in_specs=[pl.BlockSpec(memory_space=pltpu.HBM)] * 2,
        out_specs=[pl.BlockSpec(memory_space=pltpu.VMEM)] * len(cuts),
        out_shape=[pltpu.VMEM((rows, width), inverse_rows.dtype) for _, _, width in cuts],
        scratch_shapes=[pltpu.SemaphoreType.DMA((len(cuts),))],
        compiler_params=pltpu.CompilerParams(vmem_limit_bytes=VMEM_LIMIT),
        name="resident",
    )(inverse_rows, update_rows)


def opening(plan, live, right_side):
    def kernel(live_hbm, side_hbm, copies_ref, pieces_ref, lives_ref, live_ref, side_ref, sems):
        fetch_side = pltpu.make_async_copy(side_hbm, side_ref, sems.at[0])
        fetch_live = pltpu.make_async_copy(live_hbm, live_ref, sems.at[1])
        fetch_side.start()
        fetch_live.start()
        fetch_side.wait()
        for height in range(plan.levels):
            columns = pl.ds(height * plan.rows, plan.rows)
            for vector in range(plan.vectors):
                pieces_ref[height, pl.ds(vector, 1), :] = side_ref[vector, 0, :, columns]
        for block in range(plan.block_count):
            copies_ref[block] = pieces_ref[0]
        fetch_live.wait()
        for height in range(plan.levels):
            offset = 2 * plan.leaf_count - (2 * plan.leaf_count >> height)
            count = live_ref[offset + (lax.axis_index("leaf") >> height)]
            lives_ref[height] = jnp.full((plan.vectors, plan.rows), count, jnp.int32)

    tile = (plan.vectors, plan.rows)
    levels = (plan.levels, *tile)
    outs = [((plan.block_count, *tile), F32), (levels, F32), (levels, jnp.int32)]
    return pl.pallas_call(
        kernel,
        in_specs=[pl.BlockSpec(memory_space=pltpu.HBM)] * 2,
        out_specs=[pl.BlockSpec(memory_space=pltpu.VMEM)] * len(outs),
        out_shape=[pltpu.VMEM(shape, kind) for shape, kind in outs],
        scratch_shapes=[
            pltpu.SMEM(live.shape, live.dtype),
            pltpu.VMEM(right_side.shape, F32),
            pltpu.SemaphoreType.DMA((2,)),
        ],
        compiler_params=pltpu.CompilerParams(vmem_limit_bytes=VMEM_LIMIT),
        name="opening",
    )(live, right_side)


def forward_step(plan, height, live, source, inverse, pieces, update, seed):
    top = height == plan.levels - 1
    above = height if top else height + 1
    count = len(source)

    def kernel(live_ref, *refs):
        source_refs = refs[:count]
        inverse_ref = refs[count]
        y_ref, outs = refs[-1 - len(plan.spread_out(above))], refs[-len(plan.spread_out(above)) :]
        reduced = jnp.concatenate(plan.masked(live_ref, height, source_refs), axis=1).astype(BF16)
        own = plan.own_mask(live_ref, height)
        solved = own * lax.dot_general(reduced, inverse_ref[...], LAST, preferred_element_type=F32)
        y_ref[...] = solved
        rounded = (own * solved).astype(BF16)
        for (start, width), out_ref in zip(plan.ranges(above), outs):
            columns = pl.ds(start, width)
            if top:
                out_ref[...] = jnp.dot(rounded, inverse_ref[:, columns], preferred_element_type=F32)
                continue
            pieces_ref, update_ref = refs[count + 1], refs[count + 2]
            product = jnp.dot(rounded, update_ref[:, columns], preferred_element_type=F32)
            total = -product if seed is None else -refs[count + 3][:, columns] - product
            out_ref[...] = plan.slotted(pieces_ref[above], above, start, total)

    arguments = [live, *source, inverse]
    if not top:
        arguments += [pieces, update] + ([] if seed is None else [seed])
    tile = (plan.vectors, plan.rows)
    outs = [(tile, F32)] + [(shape, F32) for shape in plan.spread_out(above)]
    return call(kernel, f"forward{height}", outs, arguments)


def seed_step(plan, live, solved, update, seed):
    def kernel(live_ref, solved_ref, update_ref, *rest):
        product = jnp.dot(solved_ref[...].astype(BF16), update_ref[...], preferred_element_type=F32)
        rest[-1][...] = product if seed is None else rest[0][...] + product

    arguments = [live, solved, update] + ([] if seed is None else [seed])
    return call(kernel, "seed", [((plan.vectors, update.shape[1]), F32)], arguments)[0]


def backward_step(plan, height, live, source, residual, update, inverse):
    above = height + 1
    count = len(source)
    tile = (plan.vectors, plan.rows)
    if height == 0:
        out_shapes = [(plan.block_count, *tile)]
    else:
        out_shapes = plan.spread_out(height)

    def kernel(live_ref, *refs):
        residual_ref, update_ref, inverse_ref = refs[count : count + 3]
        x_ref = refs[count + 3]
        outs = refs[count + 4 :]
        found = plan.masked(live_ref, above, refs[:count])
        rounded = jnp.concatenate(found, axis=1).astype(BF16)
        if height > 0:
            outs[-1][...] = rounded
        rest = residual_ref[...] - lax.dot_general(
            rounded, update_ref[...], LAST, preferred_element_type=F32
        )
        weighted = (plan.own_mask(live_ref, height) * rest).astype(BF16)
        if height == 0:
            product = jnp.dot(weighted, inverse_ref[...], preferred_element_type=F32)
            for block in range(plan.block_count):
                outs[0][block] = product[:, block * plan.rows : (block + 1) * plan.rows]
        else:
            for (start, width), out_ref in zip(plan.ranges(height), outs):
                out_ref[...] = jnp.dot(weighted, inverse_ref[:, pl.ds(start, width)], preferred_element_type=F32)
        ids = jnp.full((plan.vectors, plan.rows), plan.position(above), jnp.int32)
        total = found[0]
        for block in range(1, len(found)):
            total = jnp.where(ids == block, found[block], total)
        x_ref[...] = total

    outs = [(tile, F32)] + [(shape, F32) for shape in out_shapes]
    if height > 0:
        outs.append(((plan.vectors, plan.orders[above]), BF16))
    return call(kernel, f"backward{height}", outs, [live, *source, residual, update, inverse])


def residual_step(plan, live, residual, hat, update):
    def kernel(live_ref, residual_ref, hat_ref, update_ref, out_ref):
        out_ref[...] = residual_ref[...] - lax.dot_general(
            hat_ref[...], update_ref[...], LAST, preferred_element_type=F32
        )

    return call(kernel, "residual", [(residual.shape, F32)], [live, residual, hat, update])[0]


def closing(plan, live, partials, forward, backward):
    levels = plan.levels

    def kernel(live_ref, partial_ref, *refs):
        ys, xs = refs[:levels], refs[levels : 2 * levels - 1]
        forward_ref, backward_ref = refs[2 * levels - 1 :]
        total = partial_ref[0]
        for block in range(1, plan.block_count):
            total = total + partial_ref[block]
        lowest = plan.own_mask(live_ref, 0) * total
        for height in range(levels):
            columns = pl.ds(height * plan.rows, plan.rows)
            y = ys[height][...]
            x = lowest if height == 0 else xs[height - 1][...]
            for vector in range(plan.vectors):
                forward_ref[vector, 0, :, columns] = y[vector : vector + 1]
                backward_ref[vector, 0, :, columns] = x[vector : vector + 1]

    shape = jax.ShapeDtypeStruct((plan.vectors, 1, 1, levels * plan.rows), F32)
    arguments = [live, partials, *forward, *backward]
    return pl.pallas_call(
        kernel,
        in_specs=[pl.BlockSpec(memory_space=pltpu.VMEM)] * len(arguments),
        out_specs=[pl.BlockSpec(memory_space=pltpu.VMEM)] * 2,
        out_shape=[shape, shape],
        compiler_params=pltpu.CompilerParams(vmem_limit_bytes=VMEM_LIMIT),
        name="closing",
    )(*arguments)


def local(right_side, diag_inverse, update_factor, live):
    right_side, diag_inverse, update_factor, live = (
        pltpu.with_memory_space_constraint(array, pltpu.HBM)
        for array in (right_side, diag_inverse, update_factor, live)
    )
    block_rows = diag_inverse.shape[2]
    plan = Plan(right_side.shape[0], block_rows)
    levels, orders = plan.levels, plan.orders
    inverse_cuts, update_cuts, pairs = [], [], []
    cursor = 0
    for height in range(levels):
        inverse_cuts.append((sum(orders[:height]), orders[height]))
        for ancestor in range(height + 1, levels):
            pairs.append((ancestor, height))
            update_cuts.append((cursor, orders[ancestor]))
            cursor += orders[ancestor]
    copies, pieces, live = opening(plan, live, right_side)
    held = resident(diag_inverse, update_factor, inverse_cuts, update_cuts)
    inverses = held[:levels]
    updates = dict(zip(pairs, held[levels:]))

    source = (lax.all_to_all(copies, "blk", 0, 0, tiled=True),)
    forward = []
    seeds = {}
    for height in range(levels):
        solved, *sent = forward_step(
            plan, height, live, source, inverses[height], pieces,
            updates.get((height + 1, height)), seeds.get(height + 1),
        )
        forward.append(solved)
        source = group_sum(sent, min(height + 1, levels - 1))
        for ancestor in range(height + 2, levels):
            seeds[ancestor] = seed_step(plan, live, solved, updates[ancestor, height], seeds.get(ancestor))
    residuals = list(forward)
    backward = [None] * levels
    for height in reversed(range(levels - 1)):
        above = height + 1
        backward[above], *sent = backward_step(
            plan, height, live, source, residuals[height], updates[above, height], inverses[height]
        )
        hat = sent.pop() if height > 0 else None
        for lower in range(height):
            residuals[lower] = residual_step(plan, live, residuals[lower], hat, updates[above, lower])
        if height > 0:
            source = group_sum(sent, height)
    partials = lax.all_to_all(sent[0], "blk", 0, 0, tiled=True)
    return tuple(closing(plan, live, partials, forward, backward[1:]))


def solution(mesh):
    in_specs = (
        P(None, "leaf", "blk", None),
        P("leaf", "blk", None, None),
        P("leaf", "blk", None, None),
        P(),
    )
    out_specs = (P(None, "leaf", "blk", None), P(None, "leaf", "blk", None))
    return jax.shard_map(local, mesh=mesh, in_specs=in_specs, out_specs=out_specs, check_vma=False)
```

time: 100 us -> 91.1 us (0.911)
  matrix products: 12.6 us -> 0 us
  blocking collectives: 0 us -> 9.23 us
  Pallas kernels: 0 us -> 8.18 us
  starting transfers between devices: 17.3 us -> 13.4 us
  local copies, waits for them, and re-layouts: 4.11 us -> 0.98 us
  waiting for transfers between devices: 60.2 us -> 58.1 us
  other arithmetic: 2.29 us -> 0.19 us
  between operations: 2.9 us -> 0.8 us
    dot_general x10 -> x0, matrix products: 12.6 us -> none  [the longest x3 5.21 us: local(): jnp.dot(weighted, inverses[height], preferred_element_type=jnp.float32)]
    all_to_all x0 -> x1, blocking collectives: none -> 9.23 us  [local(): partials = lax.all_to_all(sent[0], 'blk', 0, 0, tiled=True)]
    pallas_call x0 -> x10, Pallas kernels: none -> 8.18 us  [the longest x7 3.82 us: call(): pl.pallas_call(body, in_specs=[pl.BlockSpec(memory_space=pltpu.VMEM)] * l...]
    all_to_all x2 -> x1, waiting for transfers between devices: 10.3 us -> 3.24 us  [local(): source = (lax.all_to_all(copies, 'blk', 0, 0, tiled=True),)]
    ppermute x20, waiting for transfers between devices: 49.9 us -> 54.8 us  [moved(): return lax.ppermute(value, BOTH, route)]
    all_to_all x2 -> x1, starting transfers between devices: 10.6 us -> 7.32 us  [local(): source = (lax.all_to_all(copies, 'blk', 0, 0, tiled=True),)]
    convert_element_type x3 -> x0, other arithmetic: 1.97 us -> none  [local(): group_masks.append((blocks < live_count).astype(jnp.float32))]
    dynamic_slice x3 -> x0, local copies, waits for them, and re-layouts: 1.44 us -> none  [the longest x1 1.42 us: local(): live_count = live_blocks[offset + (leaf_index >> height)]]
  transfers between devices with their start and end apart: 22 -> 21, of which waited for: 21 -> 21; matrix products, arithmetic and copies ran while one was open for 6% -> 0% of each run, Pallas kernels for 0% -> 3%
where the time goes in v2:
time: 91.1 us; the launch traced here: 90.8 us
  waiting for transfers between devices  58.1 us (64%)
  starting transfers between devices  13.4 us (15%)
  blocking collectives  9.23 us (10%)
  Pallas kernels  8.18 us (9%)
  local copies, waits for them, and re-layouts  0.98 us (1%)
    ppermute x20, waiting for transfers between devices, moved(): return lax.ppermute(value, BOTH, route)  54.8 us
    all_to_all x1, blocking collectives, local(): partials = lax.all_to_all(sent[0], 'blk', 0, 0, tiled=True)  9.23 us
    all_to_all x1, starting transfers between devices, local(): source = (lax.all_to_all(copies, 'blk', 0, 0, tiled=True),)  7.32 us
    ppermute x20, starting transfers between devices, moved(): return lax.ppermute(value, BOTH, route)  6.08 us
    pallas_call x7, Pallas kernels, call(): pl.pallas_call(body, in_specs=[pl.BlockSpec(memory_space=pltpu.VMEM)] * l...  3.82 us
    all_to_all x1, waiting for transfers between devices, local(): source = (lax.all_to_all(copies, 'blk', 0, 0, tiled=True),)  3.24 us
    pallas_call x1, Pallas kernels, resident(): pl.pallas_call(kernel, in_specs=[pl.BlockSpec(memory_space=pltpu.HBM)] *...  2.34 us
  transfers between devices with their start and end apart: 21, of which 21 were waited for; matrix products, arithmetic and copies ran while one was open for 0% of the time, Pallas kernels for 3%

profile of v2, /device:TPU:0, one launch (start us, length us, event | category | flops | bytes accessed | tf_op | source)
XLA Modules:
  0.0 90.8 jit_solution(5195848580674331597)
XLA Ops:
  0.6 1.4 %opening.1 = (f32[8,4,128]{2,1,0:T(4,128)}, f32[3,4,128]{2,1,0:T(4,128)S(1)}, s32[3,4,128]{2,1,0:T(4,128)S(1)}) custom-call(s32[7]{0:T(128)} %live_hbm.1, f32[4,1,1,384]{3,2,1,0:T(1,128)} %side_hbm.1), custom_call_target="tpu_custom_call" | custom-call | tf_op jit(solution)/shard_map/opening/pallas_call | solution.py:167
  2.0 7.3 %all-to-all-start = ((f32[8,4,128]{2,1,0:T(4,128)}), f32[8,4,128]{2,1,0:T(4,128)S(1)}, u32[]{:S(2)}, u32[]{:S(2)}) async-start(f32[8,4,128]{2,1,0:T(4,128)} %get-tuple-element.25), calls=%async_computation | async-start | bytes 32768 | tf_op jit(solution)/shard_map/all_to_all | solution.py:323
  9.4 2.3 %resident.1 = (bf16[128,1024]{1,0:T(8,128)(2,1)S(1)}, bf16[128,2048]{1,0:T(8,128)(2,1)S(1)}, bf16[128,4096]{1,0:T(8,128)(2,1)S(1)}, bf16[128,2048]{1,0:T(8,128)(...) custom-call(bf16[1,1,128,7168]{3,2,1,0:T(8,128)(2,1)} %inverse_ref.1, ...), custom_call_target="tpu_custom_call" | custom-call | tf_op jit(solution)/shard_map/resident/pallas_call | solution.py:134
  11.7 0.0 copy-start
  11.7 1.0 %copy-done = bf16[128,4096]{1,0:T(8,128)(2,1)} copy-done((bf16[128,4096]{1,0:T(8,128)(2,1)}, bf16[128,4096]{1,0:T(8,128)(2,1)S(1)}, u32[]{:S(2)}) %copy-start) | copy-done | bytes 1048600
  12.7 3.2 %all-to-all-done.refs_0_ = f32[8,4,128]{2,1,0:T(4,128)S(1)} async-done(((f32[8,4,128]{2,1,0:T(4,128)}), f32[8,4,128]{2,1,0:T(4,128)S(1)}, u32[]{:S(2)}, u32[]{:S(2)}) %all-to-all-start) | async-done | bytes 16416 | tf_op jit(solution)/shard_map/all_to_all | solution.py:323
  15.9 0.0 copy-start.1
  15.9 0.5 forward0.1
  16.4 0.1 collective-permute-start
  16.5 1.2 %collective-permute-done = f32[4,2048]{1,0:T(4,128)S(1)} collective-permute-done((f32[4,2048]{1,0:T(4,128)S(1)}, f32[4,2048]{1,0:T(4,128)S(1)}, u32[]{:S(2)}, u32[]{:S(2)}) %collective-permute-start) | collective-permute-done | bytes 32800 | tf_op jit(solution)/shard_map/ppermute | solution.py:26
  17.7 0.4 collective-permute-start.1
  18.1 3.1 %collective-permute-done.1 = f32[4,2048]{1,0:T(4,128)S(1)} collective-permute-done((f32[4,2048]{1,0:T(4,128)S(1)}, f32[4,2048]{1,0:T(4,128)S(1)}, u32[]{:S(2)}, u32[]{:S(2)}) %collective-permute-start.1) | collective-permute-done | bytes 32800 | tf_op jit(solution)/shard_map/ppermute | solution.py:26
  21.1 0.3 collective-permute-start.2
  21.4 3.1 %collective-permute-done.2 = f32[4,2048]{1,0:T(4,128)S(1)} collective-permute-done((f32[4,2048]{1,0:T(4,128)S(1)}, f32[4,2048]{1,0:T(4,128)S(1)}, u32[]{:S(2)}, u32[]{:S(2)}) %collective-permute-start.2) | collective-permute-done | bytes 32800 | tf_op jit(solution)/shard_map/ppermute | solution.py:26
  24.6 0.4 collective-permute-start.3
  24.9 0.2 seed.1.refs_4_
  25.2 4.6 %collective-permute-done.3 = f32[4,2048]{1,0:T(4,128)S(1)} collective-permute-done((f32[4,2048]{1,0:T(4,128)S(1)}, f32[4,2048]{1,0:T(4,128)S(1)}, u32[]{:S(2)}, u32[]{:S(2)}) %collective-permute-start.3) | collective-permute-done | bytes 32800 | tf_op jit(solution)/shard_map/ppermute | solution.py:26
  29.8 0.8 forward1.1
  30.6 0.2 collective-permute-start.4
  30.7 1.1 %collective-permute-done.4 = f32[4,2048]{1,0:T(4,128)S(1)} collective-permute-done((f32[4,2048]{1,0:T(4,128)S(1)}, f32[4,2048]{1,0:T(4,128)S(1)}, u32[]{:S(2)}, u32[]{:S(2)}) %collective-permute-start.4) | collective-permute-done | bytes 32800 | tf_op jit(solution)/shard_map/ppermute | solution.py:26
  31.9 1.3 %collective-permute-start.5 = (f32[4,2048]{1,0:T(4,128)S(1)}, f32[4,2048]{1,0:T(4,128)S(1)}, u32[]{:S(2)}, u32[]{:S(2)}) collective-permute-start(f32[4,2048]{1,0:T(4,128)S(1)} %add.58), channel_id=1, source_target_pairs={{0,24},{1,25},{2,26},{3,27},{4,28},{5,29},{6,30},{7,31},{8,16},{9,... | collective-permute-start | bytes 98312 | tf_op jit(solution)/shard_map/ppermute | solution.py:26
  33.2 2.1 %collective-permute-done.5 = f32[4,2048]{1,0:T(4,128)S(1)} collective-permute-done((f32[4,2048]{1,0:T(4,128)S(1)}, f32[4,2048]{1,0:T(4,128)S(1)}, u32[]{:S(2)}, u32[]{:S(2)}) %collective-permute-start.5) | collective-permute-done | bytes 32800 | tf_op jit(solution)/shard_map/ppermute | solution.py:26
  35.3 0.3 collective-permute-start.6
  35.6 3.1 %collective-permute-done.6 = f32[4,2048]{1,0:T(4,128)S(1)} collective-permute-done((f32[4,2048]{1,0:T(4,128)S(1)}, f32[4,2048]{1,0:T(4,128)S(1)}, u32[]{:S(2)}, u32[]{:S(2)}) %collective-permute-start.6) | collective-permute-done | bytes 32800 | tf_op jit(solution)/shard_map/ppermute | solution.py:26
  38.7 0.1 collective-permute-start.7
  38.8 3.3 %collective-permute-done.7 = f32[4,2048]{1,0:T(4,128)S(1)} collective-permute-done((f32[4,2048]{1,0:T(4,128)S(1)}, f32[4,2048]{1,0:T(4,128)S(1)}, u32[]{:S(2)}, u32[]{:S(2)}) %collective-permute-start.7) | collective-permute-done | bytes 32800 | tf_op jit(solution)/shard_map/ppermute | solution.py:26
  42.1 0.1 collective-permute-start.8
  42.2 4.8 %collective-permute-done.8 = f32[4,2048]{1,0:T(4,128)S(1)} collective-permute-done((f32[4,2048]{1,0:T(4,128)S(1)}, f32[4,2048]{1,0:T(4,128)S(1)}, u32[]{:S(2)}, u32[]{:S(2)}) %collective-permute-start.8) | collective-permute-done | bytes 32800 | tf_op jit(solution)/shard_map/ppermute | solution.py:26
  47.0 0.2 collective-permute-start.9
  47.2 1.1 %collective-permute-done.9.refs_1_ = f32[4,2048]{1,0:T(4,128)S(1)} collective-permute-done((f32[4,2048]{1,0:T(4,128)S(1)}, f32[4,2048]{1,0:T(4,128)S(1)}, u32[]{:S(2)}, u32[]{:S(2)}) %collective-permute-start.9) | collective-permute-done | bytes 32800 | tf_op jit(solution)/shard_map/ppermute | solution.py:26
  48.3 0.0 copy-done.1
  48.3 0.9 forward2.1
  49.2 0.2 collective-permute-start.10
  49.4 1.0 %collective-permute-done.10 = f32[4,2048]{1,0:T(4,128)S(1)} collective-permute-done((f32[4,2048]{1,0:T(4,128)S(1)}, f32[4,2048]{1,0:T(4,128)S(1)}, u32[]{:S(2)}, u32[]{:S(2)}) %collective-permute-start.10) | collective-permute-done | bytes 32800 | tf_op jit(solution)/shard_map/ppermute | solution.py:26
  50.4 1.3 %collective-permute-start.11 = (f32[4,2048]{1,0:T(4,128)S(1)}, f32[4,2048]{1,0:T(4,128)S(1)}, u32[]{:S(2)}, u32[]{:S(2)}) collective-permute-start(f32[4,2048]{1,0:T(4,128)S(1)} %add.63), channel_id=1, source_target_pairs={{0,24},{1,25},{2,26},{3,27},{4,28},{5,29},{6,30},{7,31},{8,16},{9,... | collective-permute-start | bytes 98312 | tf_op jit(solution)/shard_map/ppermute | solution.py:26
  51.8 2.1 %collective-permute-done.11 = f32[4,2048]{1,0:T(4,128)S(1)} collective-permute-done((f32[4,2048]{1,0:T(4,128)S(1)}, f32[4,2048]{1,0:T(4,128)S(1)}, u32[]{:S(2)}, u32[]{:S(2)}) %collective-permute-start.11) | collective-permute-done | bytes 32800 | tf_op jit(solution)/shard_map/ppermute | solution.py:26
  53.9 0.3 collective-permute-start.12
  54.2 3.1 %collective-permute-done.12 = f32[4,2048]{1,0:T(4,128)S(1)} collective-permute-done((f32[4,2048]{1,0:T(4,128)S(1)}, f32[4,2048]{1,0:T(4,128)S(1)}, u32[]{:S(2)}, u32[]{:S(2)}) %collective-permute-start.12) | collective-permute-done | bytes 32800 | tf_op jit(solution)/shard_map/ppermute | solution.py:26
  57.3 0.1 collective-permute-start.13
  57.4 3.3 %collective-permute-done.13 = f32[4,2048]{1,0:T(4,128)S(1)} collective-permute-done((f32[4,2048]{1,0:T(4,128)S(1)}, f32[4,2048]{1,0:T(4,128)S(1)}, u32[]{:S(2)}, u32[]{:S(2)}) %collective-permute-start.13) | collective-permute-done | bytes 32800 | tf_op jit(solution)/shard_map/ppermute | solution.py:26
  60.7 0.1 collective-permute-start.14
  60.8 4.8 %collective-permute-done.14 = f32[4,2048]{1,0:T(4,128)S(1)} collective-permute-done((f32[4,2048]{1,0:T(4,128)S(1)}, f32[4,2048]{1,0:T(4,128)S(1)}, u32[]{:S(2)}, u32[]{:S(2)}) %collective-permute-start.14) | collective-permute-done | bytes 32800 | tf_op jit(solution)/shard_map/ppermute | solution.py:26
  65.6 0.2 collective-permute-start.15
  65.8 1.1 %collective-permute-done.15.refs_1_ = f32[4,2048]{1,0:T(4,128)S(1)} collective-permute-done((f32[4,2048]{1,0:T(4,128)S(1)}, f32[4,2048]{1,0:T(4,128)S(1)}, u32[]{:S(2)}, u32[]{:S(2)}) %collective-permute-start.15) | collective-permute-done | bytes 32800 | tf_op jit(solution)/shard_map/ppermute | solution.py:26
  66.9 0.7 backward1.1
  67.5 0.2 collective-permute-start.16
  67.8 1.0 %collective-permute-done.16 = f32[4,2048]{1,0:T(4,128)S(1)} collective-permute-done((f32[4,2048]{1,0:T(4,128)S(1)}, f32[4,2048]{1,0:T(4,128)S(1)}, u32[]{:S(2)}, u32[]{:S(2)}) %collective-permute-start.16) | collective-permute-done | bytes 32800 | tf_op jit(solution)/shard_map/ppermute | solution.py:26
  68.8 0.3 collective-permute-start.17
  69.1 3.1 %collective-permute-done.17 = f32[4,2048]{1,0:T(4,128)S(1)} collective-permute-done((f32[4,2048]{1,0:T(4,128)S(1)}, f32[4,2048]{1,0:T(4,128)S(1)}, u32[]{:S(2)}, u32[]{:S(2)}) %collective-permute-start.17) | collective-permute-done | bytes 32800 | tf_op jit(solution)/shard_map/ppermute | solution.py:26
  72.2 0.1 collective-permute-start.18
  72.3 3.3 %collective-permute-done.18 = f32[4,2048]{1,0:T(4,128)S(1)} collective-permute-done((f32[4,2048]{1,0:T(4,128)S(1)}, f32[4,2048]{1,0:T(4,128)S(1)}, u32[]{:S(2)}, u32[]{:S(2)}) %collective-permute-start.18) | collective-permute-done | bytes 32800 | tf_op jit(solution)/shard_map/ppermute | solution.py:26
  75.7 0.1 collective-permute-start.19
  75.7 0.4 residual.1.refs_1_
  76.1 4.4 %collective-permute-done.19 = f32[4,2048]{1,0:T(4,128)S(1)} collective-permute-done((f32[4,2048]{1,0:T(4,128)S(1)}, f32[4,2048]{1,0:T(4,128)S(1)}, u32[]{:S(2)}, u32[]{:S(2)}) %collective-permute-start.19) | collective-permute-done | bytes 32800 | tf_op jit(solution)/shard_map/ppermute | solution.py:26
  80.6 0.4 backward0.1
  81.0 9.2 %all_to_all.10.partial_ref = f32[8,4,128]{2,1,0:T(4,128)S(1)} all-to-all(f32[8,4,128]{2,1,0:T(4,128)S(1)} %get-tuple-element.42), channel_id=1, replica_groups=mesh['leaf'=4,'blk'=8] {'blk'}, dimensions={0} | all-to-all | bytes 32768 | tf_op jit(solution)/shard_map/all_to_all | solution.py:347
  90.2 0.6 closing.1
  (18 shorter events, 0.2 us)
Async XLA Ops:
  2.0 13.9 %all-to-all-start = ((f32[8,4,128]{2,1,0:T(4,128)}), f32[8,4,128]{2,1,0:T(4,128)S(1)}, u32[]{:S(2)}, u32[]{:S(2)}) async-start(f32[8,4,128]{2,1,0:T(4,128)} %get-tuple-element.25), calls=%async_computation | async-start | bytes 32768 | tf_op jit(solution)/shard_map/all_to_all | solution.py:323
  11.7 1.0 %copy-start = (bf16[128,4096]{1,0:T(8,128)(2,1)}, bf16[128,4096]{1,0:T(8,128)(2,1)S(1)}, u32[]{:S(2)}) copy-start(bf16[128,4096]{1,0:T(8,128)(2,1)S(1)} %get-tuple-element.36.refs_2_) | copy-start | bytes 3145732
  15.9 32.3 %copy-start.1 = (bf16[128,4096]{1,0:T(8,128)(2,1)S(1)}, bf16[128,4096]{1,0:T(8,128)(2,1)}, u32[]{:S(2)}) copy-start(bf16[128,4096]{1,0:T(8,128)(2,1)} %copy-done) | copy-start | bytes 3145732
  16.4 1.3 %collective-permute-start = (f32[4,2048]{1,0:T(4,128)S(1)}, f32[4,2048]{1,0:T(4,128)S(1)}, u32[]{:S(2)}, u32[]{:S(2)}) collective-permute-start(f32[4,2048]{1,0:T(4,128)S(1)} %get-tuple-element.29), channel_id=1, source_target_pairs={{0,8},{1,9},{2,10},{3,11},{4,12},{5,13},{6,14},{7,15},{8,0},{9,1},... | collective-permute-start | bytes 98312 | tf_op jit(solution)/shard_map/ppermute | solution.py:26
  17.7 3.4 %collective-permute-start.1 = (f32[4,2048]{1,0:T(4,128)S(1)}, f32[4,2048]{1,0:T(4,128)S(1)}, u32[]{:S(2)}, u32[]{:S(2)}) collective-permute-start(f32[4,2048]{1,0:T(4,128)S(1)} %add.54), channel_id=1, source_target_pairs={{0,9},{1,8},{2,11},{3,10},{4,13},{5,12},{6,15},{7,14},{8,1},{9,0},... | collective-permute-start | bytes 98312 | tf_op jit(solution)/shard_map/ppermute | solution.py:26
  21.1 3.4 %collective-permute-start.2 = (f32[4,2048]{1,0:T(4,128)S(1)}, f32[4,2048]{1,0:T(4,128)S(1)}, u32[]{:S(2)}, u32[]{:S(2)}) collective-permute-start(f32[4,2048]{1,0:T(4,128)S(1)} %add.55), channel_id=1, source_target_pairs={{0,10},{1,11},{2,8},{3,9},{4,14},{5,15},{6,12},{7,13},{8,2},{9,3},... | collective-permute-start | bytes 98312 | tf_op jit(solution)/shard_map/ppermute | solution.py:26
  24.6 5.2 %collective-permute-start.3 = (f32[4,2048]{1,0:T(4,128)S(1)}, f32[4,2048]{1,0:T(4,128)S(1)}, u32[]{:S(2)}, u32[]{:S(2)}) collective-permute-start(f32[4,2048]{1,0:T(4,128)S(1)} %add.56), channel_id=1, source_target_pairs={{0,12},{1,13},{2,14},{3,15},{4,8},{5,9},{6,10},{7,11},{8,4},{9,5},... | collective-permute-start | bytes 98312 | tf_op jit(solution)/shard_map/ppermute | solution.py:26
  30.6 1.3 %collective-permute-start.4 = (f32[4,2048]{1,0:T(4,128)S(1)}, f32[4,2048]{1,0:T(4,128)S(1)}, u32[]{:S(2)}, u32[]{:S(2)}) collective-permute-start(f32[4,2048]{1,0:T(4,128)S(1)} %get-tuple-element.35), channel_id=1, source_target_pairs={{0,8},{1,9},{2,10},{3,11},{4,12},{5,13},{6,14},{7,15},{8,0},{9,1},... | collective-permute-start | bytes 98312 | tf_op jit(solution)/shard_map/ppermute | solution.py:26
  31.9 3.4 %collective-permute-start.5 = (f32[4,2048]{1,0:T(4,128)S(1)}, f32[4,2048]{1,0:T(4,128)S(1)}, u32[]{:S(2)}, u32[]{:S(2)}) collective-permute-start(f32[4,2048]{1,0:T(4,128)S(1)} %add.58), channel_id=1, source_target_pairs={{0,24},{1,25},{2,26},{3,27},{4,28},{5,29},{6,30},{7,31},{8,16},{9,... | collective-permute-start | bytes 98312 | tf_op jit(solution)/shard_map/ppermute | solution.py:26
  35.3 3.4 %collective-permute-start.6 = (f32[4,2048]{1,0:T(4,128)S(1)}, f32[4,2048]{1,0:T(4,128)S(1)}, u32[]{:S(2)}, u32[]{:S(2)}) collective-permute-start(f32[4,2048]{1,0:T(4,128)S(1)} %add.59), channel_id=1, source_target_pairs={{0,9},{1,8},{2,11},{3,10},{4,13},{5,12},{6,15},{7,14},{8,1},{9,0},... | collective-permute-start | bytes 98312 | tf_op jit(solution)/shard_map/ppermute | solution.py:26
  38.7 3.4 %collective-permute-start.7 = (f32[4,2048]{1,0:T(4,128)S(1)}, f32[4,2048]{1,0:T(4,128)S(1)}, u32[]{:S(2)}, u32[]{:S(2)}) collective-permute-start(f32[4,2048]{1,0:T(4,128)S(1)} %add.60), channel_id=1, source_target_pairs={{0,10},{1,11},{2,8},{3,9},{4,14},{5,15},{6,12},{7,13},{8,2},{9,3},... | collective-permute-start | bytes 98312 | tf_op jit(solution)/shard_map/ppermute | solution.py:26
  42.1 4.9 %collective-permute-start.8 = (f32[4,2048]{1,0:T(4,128)S(1)}, f32[4,2048]{1,0:T(4,128)S(1)}, u32[]{:S(2)}, u32[]{:S(2)}) collective-permute-start(f32[4,2048]{1,0:T(4,128)S(1)} %add.61), channel_id=1, source_target_pairs={{0,12},{1,13},{2,14},{3,15},{4,8},{5,9},{6,10},{7,11},{8,4},{9,5},... | collective-permute-start | bytes 98312 | tf_op jit(solution)/shard_map/ppermute | solution.py:26
  47.0 1.3 %collective-permute-start.9 = (f32[4,2048]{1,0:T(4,128)S(1)}, f32[4,2048]{1,0:T(4,128)S(1)}, u32[]{:S(2)}, u32[]{:S(2)}) collective-permute-start(f32[4,2048]{1,0:T(4,128)S(1)} %add.62.refs_0_), channel_id=1, source_target_pairs={{0,8},{1,9},{2,10},{3,11},{4,12},{5,13},{6,14},{7,15},{8,0},{9,1},... | collective-permute-start | bytes 98312 | tf_op jit(solution)/shard_map/ppermute | solution.py:26
  49.2 1.3 %collective-permute-start.10 = (f32[4,2048]{1,0:T(4,128)S(1)}, f32[4,2048]{1,0:T(4,128)S(1)}, u32[]{:S(2)}, u32[]{:S(2)}) collective-permute-start(f32[4,2048]{1,0:T(4,128)S(1)} %get-tuple-element.38), channel_id=1, source_target_pairs={{0,8},{1,9},{2,10},{3,11},{4,12},{5,13},{6,14},{7,15},{8,0},{9,1},... | collective-permute-start | bytes 98312 | tf_op jit(solution)/shard_map/ppermute | solution.py:26
  50.4 3.4 %collective-permute-start.11 = (f32[4,2048]{1,0:T(4,128)S(1)}, f32[4,2048]{1,0:T(4,128)S(1)}, u32[]{:S(2)}, u32[]{:S(2)}) collective-permute-start(f32[4,2048]{1,0:T(4,128)S(1)} %add.63), channel_id=1, source_target_pairs={{0,24},{1,25},{2,26},{3,27},{4,28},{5,29},{6,30},{7,31},{8,16},{9,... | collective-permute-start | bytes 98312 | tf_op jit(solution)/shard_map/ppermute | solution.py:26
  53.9 3.4 %collective-permute-start.12 = (f32[4,2048]{1,0:T(4,128)S(1)}, f32[4,2048]{1,0:T(4,128)S(1)}, u32[]{:S(2)}, u32[]{:S(2)}) collective-permute-start(f32[4,2048]{1,0:T(4,128)S(1)} %add.64), channel_id=1, source_target_pairs={{0,9},{1,8},{2,11},{3,10},{4,13},{5,12},{6,15},{7,14},{8,1},{9,0},... | collective-permute-start | bytes 98312 | tf_op jit(solution)/shard_map/ppermute | solution.py:26
  57.3 3.4 %collective-permute-start.13 = (f32[4,2048]{1,0:T(4,128)S(1)}, f32[4,2048]{1,0:T(4,128)S(1)}, u32[]{:S(2)}, u32[]{:S(2)}) collective-permute-start(f32[4,2048]{1,0:T(4,128)S(1)} %add.65), channel_id=1, source_target_pairs={{0,10},{1,11},{2,8},{3,9},{4,14},{5,15},{6,12},{7,13},{8,2},{9,3},... | collective-permute-start | bytes 98312 | tf_op jit(solution)/shard_map/ppermute | solution.py:26
  60.7 4.9 %collective-permute-start.14 = (f32[4,2048]{1,0:T(4,128)S(1)}, f32[4,2048]{1,0:T(4,128)S(1)}, u32[]{:S(2)}, u32[]{:S(2)}) collective-permute-start(f32[4,2048]{1,0:T(4,128)S(1)} %add.66), channel_id=1, source_target_pairs={{0,12},{1,13},{2,14},{3,15},{4,8},{5,9},{6,10},{7,11},{8,4},{9,5},... | collective-permute-start | bytes 98312 | tf_op jit(solution)/shard_map/ppermute | solution.py:26
  65.6 1.3 %collective-permute-start.15 = (f32[4,2048]{1,0:T(4,128)S(1)}, f32[4,2048]{1,0:T(4,128)S(1)}, u32[]{:S(2)}, u32[]{:S(2)}) collective-permute-start(f32[4,2048]{1,0:T(4,128)S(1)} %add.67.refs_0_), channel_id=1, source_target_pairs={{0,8},{1,9},{2,10},{3,11},{4,12},{5,13},{6,14},{7,15},{8,0},{9,1},... | collective-permute-start | bytes 98312 | tf_op jit(solution)/shard_map/ppermute | solution.py:26
  67.5 1.3 %collective-permute-start.16 = (f32[4,2048]{1,0:T(4,128)S(1)}, f32[4,2048]{1,0:T(4,128)S(1)}, u32[]{:S(2)}, u32[]{:S(2)}) collective-permute-start(f32[4,2048]{1,0:T(4,128)S(1)} %get-tuple-element.40), channel_id=1, source_target_pairs={{0,8},{1,9},{2,10},{3,11},{4,12},{5,13},{6,14},{7,15},{8,0},{9,1},... | collective-permute-start | bytes 98312 | tf_op jit(solution)/shard_map/ppermute | solution.py:26
  68.8 3.4 %collective-permute-start.17 = (f32[4,2048]{1,0:T(4,128)S(1)}, f32[4,2048]{1,0:T(4,128)S(1)}, u32[]{:S(2)}, u32[]{:S(2)}) collective-permute-start(f32[4,2048]{1,0:T(4,128)S(1)} %add.68), channel_id=1, source_target_pairs={{0,9},{1,8},{2,11},{3,10},{4,13},{5,12},{6,15},{7,14},{8,1},{9,0},... | collective-permute-start | bytes 98312 | tf_op jit(solution)/shard_map/ppermute | solution.py:26
  72.2 3.4 %collective-permute-start.18 = (f32[4,2048]{1,0:T(4,128)S(1)}, f32[4,2048]{1,0:T(4,128)S(1)}, u32[]{:S(2)}, u32[]{:S(2)}) collective-permute-start(f32[4,2048]{1,0:T(4,128)S(1)} %add.69), channel_id=1, source_target_pairs={{0,10},{1,11},{2,8},{3,9},{4,14},{5,15},{6,12},{7,13},{8,2},{9,3},... | collective-permute-start | bytes 98312 | tf_op jit(solution)/shard_map/ppermute | solution.py:26
  75.7 4.9 %collective-permute-start.19 = (f32[4,2048]{1,0:T(4,128)S(1)}, f32[4,2048]{1,0:T(4,128)S(1)}, u32[]{:S(2)}, u32[]{:S(2)}) collective-permute-start(f32[4,2048]{1,0:T(4,128)S(1)} %add.70), channel_id=1, source_target_pairs={{0,12},{1,13},{2,14},{3,15},{4,8},{5,9},{6,10},{7,11},{8,4},{9,5},... | collective-permute-start | bytes 98312 | tf_op jit(solution)/shard_map/ppermute | solution.py:26

commit v3 on v2

--- a/solution.py
+++ b/solution.py
@@ -11,6 +11,7 @@
 LAST = (((1,), (1,)), ((), ()))
 HALVE_BYTES = 65536
 VMEM_LIMIT = 8 << 20
+FIRST = ((0, 0), (1, 0))
 F32 = jnp.float32
 BF16 = jnp.bfloat16
 
@@ -26,21 +27,27 @@
     return lax.ppermute(value, BOTH, route)
 
 
-def group_moves(height):
+def group_steps(height):
     block_bits = lax.axis_size("blk").bit_length() - 1
-    return [(1 << bit | 1, 0) for bit in range(1, height)] + [(1, 1 << bit) for bit in range(block_bits)]
+    dimensions = [(1 << bit | 1, 0) for bit in range(1, height)] + [(1, 1 << bit) for bit in range(block_bits)]
+    steps = [[dimensions.pop(1)]] if len(dimensions) % 2 else []
+    return steps + [dimensions[i : i + 2] for i in range(0, len(dimensions), 2)]
+
+
+def stepped(value, step):
+    hops = list(step)
+    if len(step) == 2:
+        hops.append((step[0][0] ^ step[1][0], step[0][1] ^ step[1][1]))
+    for part in [moved(value, *hop) for hop in hops]:
+        value = value + part
+    return value
 
 
 def group_sum(values, height):
-    if len(values) == 1:
-        value = values[0] + moved(values[0], 1, 0)
-        for move in group_moves(height):
-            value = value + moved(value, *move)
-        return (value,)
-    part = values[0] + moved(values[1], 1, 0)
-    for move in group_moves(height):
-        part = part + moved(part, *move)
-    return part, moved(part, 1, 0)
+    total = values[0] + moved(values[-1], 1, 0)
+    for step in group_steps(height):
+        total = stepped(total, step)
+    return (total,) if len(values) == 1 else (total, moved(total, 1, 0))
 
 
 class Plan:
@@ -116,16 +123,18 @@
     )(*arguments)
 
 
-def resident(inverse_rows, update_rows, inverse_cuts, update_cuts):
-    cuts = [(0, *cut) for cut in inverse_cuts] + [(1, *cut) for cut in update_cuts]
-    rows = inverse_rows.shape[2]
-
-    def kernel(inverse_ref, update_ref, *rest):
-        outs, sems = rest[: len(cuts)], rest[len(cuts)]
-        copies = []
-        for index, (which, start, width) in enumerate(cuts):
-            source = (inverse_ref, update_ref)[which].at[0, 0, :, pl.ds(start, width)]
-            copies.append(pltpu.make_async_copy(source, outs[index], sems.at[index]))
+def fetched(plan, cuts, refs, outs, sems):
+    return [
+        pltpu.make_async_copy(refs[which].at[0, 0, :, pl.ds(start, width)], out, sems.at[index])
+        for index, ((which, start, width), out) in enumerate(zip(cuts, outs))
+    ]
+
+
+def resident(plan, diag_inverse, update_factor, cuts, after):
+    count = len(cuts)
+
+    def kernel(inverse_hbm, update_hbm, after_ref, *rest):
+        copies = fetched(plan, cuts, (inverse_hbm, update_hbm), rest[:count], rest[count])
         for copy in copies:
             copy.start()
         for copy in copies:
@@ -133,21 +142,27 @@
 
     return pl.pallas_call(
         kernel,
-        in_specs=[pl.BlockSpec(memory_space=pltpu.HBM)] * 2,
-        out_specs=[pl.BlockSpec(memory_space=pltpu.VMEM)] * len(cuts),
-        out_shape=[pltpu.VMEM((rows, width), inverse_rows.dtype) for _, _, width in cuts],
-        scratch_shapes=[pltpu.SemaphoreType.DMA((len(cuts),))],
+        in_specs=[pl.BlockSpec(memory_space=pltpu.HBM)] * 2 + [pl.BlockSpec(memory_space=pltpu.VMEM)],
+        out_specs=[pl.BlockSpec(memory_space=pltpu.VMEM)] * count,
+        out_shape=[pltpu.VMEM((plan.rows, width), BF16) for _, _, width in cuts],
+        scratch_shapes=[pltpu.SemaphoreType.DMA((count,))],
         compiler_params=pltpu.CompilerParams(vmem_limit_bytes=VMEM_LIMIT),
         name="resident",
-    )(inverse_rows, update_rows)
-
-
-def opening(plan, live, right_side):
-    def kernel(live_hbm, side_hbm, copies_ref, pieces_ref, lives_ref, live_ref, side_ref, sems):
+    )(diag_inverse, update_factor, after)
+
+
+def opening(plan, live, right_side, diag_inverse, update_factor, cuts):
+    count = len(cuts)
+
+    def kernel(live_hbm, side_hbm, inverse_hbm, update_hbm, copies_ref, pieces_ref, lives_ref, *rest):
+        live_ref, side_ref, sems, held_sems = rest[count:]
         fetch_side = pltpu.make_async_copy(side_hbm, side_ref, sems.at[0])
         fetch_live = pltpu.make_async_copy(live_hbm, live_ref, sems.at[1])
+        held = fetched(plan, cuts, (inverse_hbm, update_hbm), rest[:count], held_sems)
         fetch_side.start()
         fetch_live.start()
+        for copy in held:
+            copy.start()
         fetch_side.wait()
         for height in range(plan.levels):
             columns = pl.ds(height * plan.rows, plan.rows)
@@ -158,25 +173,29 @@
         fetch_live.wait()
         for height in range(plan.levels):
             offset = 2 * plan.leaf_count - (2 * plan.leaf_count >> height)
-            count = live_ref[offset + (lax.axis_index("leaf") >> height)]
-            lives_ref[height] = jnp.full((plan.vectors, plan.rows), count, jnp.int32)
+            alive = live_ref[offset + (lax.axis_index("leaf") >> height)]
+            lives_ref[height] = jnp.full((plan.vectors, plan.rows), alive, jnp.int32)
+        for copy in held:
+            copy.wait()
 
     tile = (plan.vectors, plan.rows)
     levels = (plan.levels, *tile)
     outs = [((plan.block_count, *tile), F32), (levels, F32), (levels, jnp.int32)]
+    outs += [((plan.rows, width), BF16) for _, _, width in cuts]
     return pl.pallas_call(
         kernel,
-        in_specs=[pl.BlockSpec(memory_space=pltpu.HBM)] * 2,
+        in_specs=[pl.BlockSpec(memory_space=pltpu.HBM)] * 4,
         out_specs=[pl.BlockSpec(memory_space=pltpu.VMEM)] * len(outs),
         out_shape=[pltpu.VMEM(shape, kind) for shape, kind in outs],
         scratch_shapes=[
             pltpu.SMEM(live.shape, live.dtype),
             pltpu.VMEM(right_side.shape, F32),
             pltpu.SemaphoreType.DMA((2,)),
+            pltpu.SemaphoreType.DMA((count,)),
         ],
         compiler_params=pltpu.CompilerParams(vmem_limit_bytes=VMEM_LIMIT),
         name="opening",
-    )(live, right_side)
+    )(live, right_side, diag_inverse, update_factor)
 
 
 def forward_step(plan, height, live, source, inverse, pieces, update, seed):
@@ -307,41 +326,43 @@
     block_rows = diag_inverse.shape[2]
     plan = Plan(right_side.shape[0], block_rows)
     levels, orders = plan.levels, plan.orders
-    inverse_cuts, update_cuts, pairs = [], [], []
+    cuts = {(height, height): (0, sum(orders[:height]), orders[height]) for height in range(levels)}
     cursor = 0
     for height in range(levels):
-        inverse_cuts.append((sum(orders[:height]), orders[height]))
         for ancestor in range(height + 1, levels):
-            pairs.append((ancestor, height))
-            update_cuts.append((cursor, orders[ancestor]))
+            cuts[ancestor, height] = (1, cursor, orders[ancestor])
             cursor += orders[ancestor]
-    copies, pieces, live = opening(plan, live, right_side)
-    held = resident(diag_inverse, update_factor, inverse_cuts, update_cuts)
-    inverses = held[:levels]
-    updates = dict(zip(pairs, held[levels:]))
-
+    first = [key for key in cuts if key in FIRST]
+    later = [key for key in cuts if key not in FIRST]
+    copies, pieces, live, *held = opening(
+        plan, live, right_side, diag_inverse, update_factor, [cuts[key] for key in first]
+    )
+    matrices = dict(zip(first, held))
     source = (lax.all_to_all(copies, "blk", 0, 0, tiled=True),)
     forward = []
     seeds = {}
     for height in range(levels):
         solved, *sent = forward_step(
-            plan, height, live, source, inverses[height], pieces,
-            updates.get((height + 1, height)), seeds.get(height + 1),
+            plan, height, live, source, matrices[height, height], pieces,
+            matrices.get((height + 1, height)), seeds.get(height + 1),
         )
         forward.append(solved)
+        if height == 0:
+            held = resident(plan, diag_inverse, update_factor, [cuts[key] for key in later], solved)
+            matrices.update(zip(later, held))
         source = group_sum(sent, min(height + 1, levels - 1))
         for ancestor in range(height + 2, levels):
-            seeds[ancestor] = seed_step(plan, live, solved, updates[ancestor, height], seeds.get(ancestor))
+            seeds[ancestor] = seed_step(plan, live, solved, matrices[ancestor, height], seeds.get(ancestor))
     residuals = list(forward)
     backward = [None] * levels
     for height in reversed(range(levels - 1)):
         above = height + 1
         backward[above], *sent = backward_step(
-            plan, height, live, source, residuals[height], updates[above, height], inverses[height]
+            plan, height, live, source, residuals[height], matrices[above, height], matrices[height, height]
         )
         hat = sent.pop() if height > 0 else None
         for lower in range(height):
-            residuals[lower] = residual_step(plan, live, residuals[lower], hat, updates[above, lower])
+            residuals[lower] = residual_step(plan, live, residuals[lower], hat, matrices[above, lower])
         if height > 0:
             source = group_sum(sent, height)
     partials = lax.all_to_all(sent[0], "blk", 0, 0, tiled=True)

time: 91.1 us -> 82.3 us (0.903)
  waiting for transfers between devices: 58.1 us -> 25.5 us
  blocking collectives: 9.23 us -> 22.9 us
  starting transfers between devices: 13.4 us -> 25.1 us
  local copies, waits for them, and re-layouts: 0.98 us -> 0 us
    ppermute x20 -> x26, waiting for transfers between devices: 54.8 us -> 25.5 us  [moved(): return lax.ppermute(value, BOTH, route)]
    ppermute x20 -> x26, starting transfers between devices: 6.08 us -> 25.1 us  [moved(): return lax.ppermute(value, BOTH, route)]
    all_to_all x0 -> x1, blocking collectives: none -> 13.7 us  [local(): source = (lax.all_to_all(copies, 'blk', 0, 0, tiled=True),)]
    all_to_all x1 -> x0, starting transfers between devices: 7.32 us -> none  [local(): source = (lax.all_to_all(copies, 'blk', 0, 0, tiled=True),)]
    all_to_all x1 -> x0, waiting for transfers between devices: 3.24 us -> none  [local(): source = (lax.all_to_all(copies, 'blk', 0, 0, tiled=True),)]
    unnamed x4 -> x0, local copies, waits for them, and re-layouts: 0.98 us -> none
  transfers between devices with their start and end apart: 21 -> 26, of which waited for: 21 -> 20; matrix products, arithmetic and copies ran while one was open for 0% -> 0% of each run, Pallas kernels for 3% -> 3%
where the time goes in v3:
time: 82.3 us; the launch traced here: 82.1 us
  waiting for transfers between devices  25.5 us (31%)
  starting transfers between devices  25.1 us (30%)
  blocking collectives  22.9 us (28%)
  Pallas kernels  7.71 us (9%)
    ppermute x26, waiting for transfers between devices, moved(): return lax.ppermute(value, BOTH, route)  25.5 us
    ppermute x26, starting transfers between devices, moved(): return lax.ppermute(value, BOTH, route)  25.1 us
    all_to_all x1, blocking collectives, local(): source = (lax.all_to_all(copies, 'blk', 0, 0, tiled=True),)  13.7 us
    all_to_all x1, blocking collectives, local(): partials = lax.all_to_all(sent[0], 'blk', 0, 0, tiled=True)  9.24 us
    pallas_call x7, Pallas kernels, call(): pl.pallas_call(body, in_specs=[pl.BlockSpec(memory_space=pltpu.VMEM)] * l...  3.82 us
    pallas_call x1, Pallas kernels, resident(): pl.pallas_call(kernel, in_specs=[pl.BlockSpec(memory_space=pltpu.HBM)] *...  2.1 us
  transfers between devices with their start and end apart: 26, of which 20 were waited for; matrix products, arithmetic and copies ran while one was open for 0% of the time, Pallas kernels for 3%

profile of v3, /device:TPU:0, one launch (start us, length us, event | category | flops | bytes accessed | tf_op | source)
XLA Modules:
  0.0 82.1 jit_solution(9712899853553138073)
XLA Ops:
  0.6 1.2 %opening.1 = (f32[8,4,128]{2,1,0:T(4,128)S(1)}, f32[3,4,128]{2,1,0:T(4,128)S(1)}, s32[3,4,128]{2,1,0:T(4,128)S(1)}, bf16[128,1024]{1,0:T(8,128)(2,1)S(1)}, bf16[128,2048]{1,0:T(8,128)(2,1)S(1)}) custom-call(s32[7]{0:T(128)} %live_hbm.1, f32[4,1,1,384]{3,2,1,0:T(1,128)} %side_hbm.1, bf16[1,1,128,7168]{3,2,1,0:T(8,128)(2,1)} %inverse_hbm.3, ...), custom_call_target="tpu_custom_call" | custom-call | tf_op jit(solution)/shard_map/opening/pallas_call | solution.py:185
  1.8 13.7 %all_to_all.10.refs_0_ = f32[8,4,128]{2,1,0:T(4,128)S(1)} all-to-all(f32[8,4,128]{2,1,0:T(4,128)S(1)} %get-tuple-element.25), channel_id=1, replica_groups=mesh['leaf'=4,'blk'=8] {'blk'}, dimensions={0} | all-to-all | bytes 32768 | tf_op jit(solution)/shard_map/all_to_all | solution.py:341
  15.5 0.5 forward0.1
  16.0 0.1 collective-permute-start
  16.0 1.2 %collective-permute-done = f32[4,2048]{1,0:T(4,128)S(1)} collective-permute-done((f32[4,2048]{1,0:T(4,128)S(1)}, f32[4,2048]{1,0:T(4,128)S(1)}, u32[]{:S(2)}, u32[]{:S(2)}) %collective-permute-start) | collective-permute-done | bytes 32800 | tf_op jit(solution)/shard_map/ppermute | solution.py:27
  17.3 0.3 collective-permute-start.1
  17.6 3.1 %collective-permute-done.1 = f32[4,2048]{1,0:T(4,128)S(1)} collective-permute-done((f32[4,2048]{1,0:T(4,128)S(1)}, f32[4,2048]{1,0:T(4,128)S(1)}, u32[]{:S(2)}, u32[]{:S(2)}) %collective-permute-start.1) | collective-permute-done | bytes 32800 | tf_op jit(solution)/shard_map/ppermute | solution.py:27
  20.7 0.6 collective-permute-start.4
  21.2 1.9 %collective-permute-start.3 = (f32[4,2048]{1,0:T(4,128)S(1)}, f32[4,2048]{1,0:T(4,128)S(1)}, u32[]{:S(2)}, u32[]{:S(2)}) collective-permute-start(f32[4,2048]{1,0:T(4,128)S(1)} %add.73), channel_id=1, source_target_pairs={{0,12},{1,13},{2,14},{3,15},{4,8},{5,9},{6,10},{7,11},{8,4},{9,5},... | collective-permute-start | bytes 98312 | tf_op jit(solution)/shard_map/ppermute | solution.py:27
  23.1 1.7 %collective-permute-start.2 = (f32[4,2048]{1,0:T(4,128)S(1)}, f32[4,2048]{1,0:T(4,128)S(1)}, u32[]{:S(2)}, u32[]{:S(2)}) collective-permute-start(f32[4,2048]{1,0:T(4,128)S(1)} %add.73), channel_id=1, source_target_pairs={{0,9},{1,8},{2,11},{3,10},{4,13},{5,12},{6,15},{7,14},{8,1},{9,0},... | collective-permute-start | bytes 98312 | tf_op jit(solution)/shard_map/ppermute | solution.py:27
  24.9 2.1 %resident.1 = (bf16[128,2048]{1,0:T(8,128)(2,1)S(1)}, bf16[128,4096]{1,0:T(8,128)(2,1)S(1)}, bf16[128,4096]{1,0:T(8,128)(2,1)S(1)}, bf16[128,4096]{1,0:T(8,128)(2,1)S(1)}) custom-call(bf16[1,1,128,7168]{3,2,1,0:T(8,128)(2,1)} %inverse_hbm.3, bf16[1,1,128,10240]{3,2,1,0:T(8,128)(2,1)} %update_hbm.3, ...), custom_call_target="tpu_custom_call" | custom-call | tf_op jit(solution)/shard_map/resident/pallas_call | solution.py:143
  27.0 0.2 seed.1.refs_4_
  27.2 0.6 collective-permute-done.4
  27.8 0.0 collective-permute-done.3
  27.8 0.0 collective-permute-done.2
  27.8 0.8 forward1.1
  28.6 0.1 collective-permute-start.5
  28.6 1.2 %collective-permute-done.5 = f32[4,2048]{1,0:T(4,128)S(1)} collective-permute-done((f32[4,2048]{1,0:T(4,128)S(1)}, f32[4,2048]{1,0:T(4,128)S(1)}, u32[]{:S(2)}, u32[]{:S(2)}) %collective-permute-start.5) | collective-permute-done | bytes 32800 | tf_op jit(solution)/shard_map/ppermute | solution.py:27
  29.8 1.6 %collective-permute-start.8 = (f32[4,2048]{1,0:T(4,128)S(1)}, f32[4,2048]{1,0:T(4,128)S(1)}, u32[]{:S(2)}, u32[]{:S(2)}) collective-permute-start(f32[4,2048]{1,0:T(4,128)S(1)} %add.77), channel_id=1, source_target_pairs={{0,17},{1,16},{2,19},{3,18},{4,21},{5,20},{6,23},{7,22},{8,25},{9,... | collective-permute-start | bytes 98312 | tf_op jit(solution)/shard_map/ppermute | solution.py:27
  31.4 0.9 %collective-permute-start.7 = (f32[4,2048]{1,0:T(4,128)S(1)}, f32[4,2048]{1,0:T(4,128)S(1)}, u32[]{:S(2)}, u32[]{:S(2)}) collective-permute-start(f32[4,2048]{1,0:T(4,128)S(1)} %add.77), channel_id=1, source_target_pairs={{0,9},{1,8},{2,11},{3,10},{4,13},{5,12},{6,15},{7,14},{8,1},{9,0},... | collective-permute-start | bytes 98312 | tf_op jit(solution)/shard_map/ppermute | solution.py:27
  32.4 0.8 collective-permute-start.6
  33.1 1.6 %collective-permute-done.8 = f32[4,2048]{1,0:T(4,128)S(1)} collective-permute-done((f32[4,2048]{1,0:T(4,128)S(1)}, f32[4,2048]{1,0:T(4,128)S(1)}, u32[]{:S(2)}, u32[]{:S(2)}) %collective-permute-start.8) | collective-permute-done | bytes 32800 | tf_op jit(solution)/shard_map/ppermute | solution.py:27
  34.8 0.7 collective-permute-done.7
  35.4 0.3 collective-permute-done.6
  35.7 0.6 collective-permute-start.11
  36.4 0.8 collective-permute-start.10
  37.1 2.8 %collective-permute-start.9 = (f32[4,2048]{1,0:T(4,128)S(1)}, f32[4,2048]{1,0:T(4,128)S(1)}, u32[]{:S(2)}, u32[]{:S(2)}) collective-permute-start(f32[4,2048]{1,0:T(4,128)S(1)} %add_add_fusion.4), channel_id=1, source_target_pairs={{0,10},{1,11},{2,8},{3,9},{4,14},{5,15},{6,12},{7,13},{8,2},{9,3},... | collective-permute-start | bytes 98312 | tf_op jit(solution)/shard_map/ppermute | solution.py:27
  39.9 2.1 %collective-permute-done.11 = f32[4,2048]{1,0:T(4,128)S(1)} collective-permute-done((f32[4,2048]{1,0:T(4,128)S(1)}, f32[4,2048]{1,0:T(4,128)S(1)}, u32[]{:S(2)}, u32[]{:S(2)}) %collective-permute-start.11) | collective-permute-done | bytes 32800 | tf_op jit(solution)/shard_map/ppermute | solution.py:27
  41.9 0.0 collective-permute-done.10
  41.9 0.2 collective-permute-done.9
  42.2 0.2 collective-permute-start.12
  42.4 1.1 %collective-permute-done.12.refs_1_ = f32[4,2048]{1,0:T(4,128)S(1)} collective-permute-done((f32[4,2048]{1,0:T(4,128)S(1)}, f32[4,2048]{1,0:T(4,128)S(1)}, u32[]{:S(2)}, u32[]{:S(2)}) %collective-permute-start.12) | collective-permute-done | bytes 32800 | tf_op jit(solution)/shard_map/ppermute | solution.py:27
  43.5 0.9 %forward2.1 = (f32[4,128]{1,0:T(4,128)S(1)}, f32[4,2048]{1,0:T(4,128)S(1)}, f32[4,2048]{1,0:T(4,128)S(1)}) custom-call(s32[3,4,128]{2,1,0:T(4,128)S(1)} %get-tuple-element.24.live_ref, f32[4,2048]{1,0:T(4,128)S(1)} %add_add_fusion.3.refs_0_, f32[4,2048]{1,0:T(4,128)S(1)} %collective-permute-done.12.refs_1_, bf16[128,4096]{1,0:T(8,128)(2,1)S(1)} %get-tuple-element.36.refs_2_), custom_call_target="tpu_custom_call" | custom-call | tf_op jit(solution)/shard_map/forward2/pallas_call | solution.py:116
  44.4 0.2 collective-permute-start.13
  44.6 1.0 %collective-permute-done.13 = f32[4,2048]{1,0:T(4,128)S(1)} collective-permute-done((f32[4,2048]{1,0:T(4,128)S(1)}, f32[4,2048]{1,0:T(4,128)S(1)}, u32[]{:S(2)}, u32[]{:S(2)}) %collective-permute-start.13) | collective-permute-done | bytes 32800 | tf_op jit(solution)/shard_map/ppermute | solution.py:27
  45.6 1.8 %collective-permute-start.16 = (f32[4,2048]{1,0:T(4,128)S(1)}, f32[4,2048]{1,0:T(4,128)S(1)}, u32[]{:S(2)}, u32[]{:S(2)}) collective-permute-start(f32[4,2048]{1,0:T(4,128)S(1)} %add.84), channel_id=1, source_target_pairs={{0,17},{1,16},{2,19},{3,18},{4,21},{5,20},{6,23},{7,22},{8,25},{9,... | collective-permute-start | bytes 98312 | tf_op jit(solution)/shard_map/ppermute | solution.py:27
  47.4 0.3 collective-permute-start.15
  47.6 1.3 %collective-permute-start.14 = (f32[4,2048]{1,0:T(4,128)S(1)}, f32[4,2048]{1,0:T(4,128)S(1)}, u32[]{:S(2)}, u32[]{:S(2)}) collective-permute-start(f32[4,2048]{1,0:T(4,128)S(1)} %add.84), channel_id=1, source_target_pairs={{0,24},{1,25},{2,26},{3,27},{4,28},{5,29},{6,30},{7,31},{8,16},{9,... | collective-permute-start | bytes 98312 | tf_op jit(solution)/shard_map/ppermute | solution.py:27
  48.9 1.6 %collective-permute-done.16 = f32[4,2048]{1,0:T(4,128)S(1)} collective-permute-done((f32[4,2048]{1,0:T(4,128)S(1)}, f32[4,2048]{1,0:T(4,128)S(1)}, u32[]{:S(2)}, u32[]{:S(2)}) %collective-permute-start.16) | collective-permute-done | bytes 32800 | tf_op jit(solution)/shard_map/ppermute | solution.py:27
  50.5 0.7 collective-permute-done.15
  51.2 0.0 collective-permute-done.14
  51.2 1.7 %collective-permute-start.19 = (f32[4,2048]{1,0:T(4,128)S(1)}, f32[4,2048]{1,0:T(4,128)S(1)}, u32[]{:S(2)}, u32[]{:S(2)}) collective-permute-start(f32[4,2048]{1,0:T(4,128)S(1)} %add_add_fusion.2), channel_id=1, source_target_pairs={{0,6},{1,7},{2,4},{3,5},{4,2},{5,3},{6,0},{7,1},{8,14},{9,15},{10,... | collective-permute-start | bytes 98312 | tf_op jit(solution)/shard_map/ppermute | solution.py:27
  52.9 0.5 collective-permute-start.18
  53.4 2.0 %collective-permute-start.17 = (f32[4,2048]{1,0:T(4,128)S(1)}, f32[4,2048]{1,0:T(4,128)S(1)}, u32[]{:S(2)}, u32[]{:S(2)}) collective-permute-start(f32[4,2048]{1,0:T(4,128)S(1)} %add_add_fusion.2), channel_id=1, source_target_pairs={{0,10},{1,11},{2,8},{3,9},{4,14},{5,15},{6,12},{7,13},{8,2},{9,3},... | collective-permute-start | bytes 98312 | tf_op jit(solution)/shard_map/ppermute | solution.py:27
  55.4 1.8 %collective-permute-done.19 = f32[4,2048]{1,0:T(4,128)S(1)} collective-permute-done((f32[4,2048]{1,0:T(4,128)S(1)}, f32[4,2048]{1,0:T(4,128)S(1)}, u32[]{:S(2)}, u32[]{:S(2)}) %collective-permute-start.19) | collective-permute-done | bytes 32800 | tf_op jit(solution)/shard_map/ppermute | solution.py:27
  57.2 0.9 %collective-permute-done.18 = f32[4,2048]{1,0:T(4,128)S(1)} collective-permute-done((f32[4,2048]{1,0:T(4,128)S(1)}, f32[4,2048]{1,0:T(4,128)S(1)}, u32[]{:S(2)}, u32[]{:S(2)}) %collective-permute-start.18) | collective-permute-done | bytes 32800 | tf_op jit(solution)/shard_map/ppermute | solution.py:27
  58.2 0.0 collective-permute-done.17
  58.2 0.2 collective-permute-start.20
  58.4 1.1 %collective-permute-done.20.refs_1_ = f32[4,2048]{1,0:T(4,128)S(1)} collective-permute-done((f32[4,2048]{1,0:T(4,128)S(1)}, f32[4,2048]{1,0:T(4,128)S(1)}, u32[]{:S(2)}, u32[]{:S(2)}) %collective-permute-start.20) | collective-permute-done | bytes 32800 | tf_op jit(solution)/shard_map/ppermute | solution.py:27
  59.5 0.7 backward1.1
  60.1 0.2 collective-permute-start.21
  60.4 1.0 %collective-permute-done.21 = f32[4,2048]{1,0:T(4,128)S(1)} collective-permute-done((f32[4,2048]{1,0:T(4,128)S(1)}, f32[4,2048]{1,0:T(4,128)S(1)}, u32[]{:S(2)}, u32[]{:S(2)}) %collective-permute-start.21) | collective-permute-done | bytes 32800 | tf_op jit(solution)/shard_map/ppermute | solution.py:27
  61.4 0.6 collective-permute-start.22
  62.0 2.8 %collective-permute-done.22 = f32[4,2048]{1,0:T(4,128)S(1)} collective-permute-done((f32[4,2048]{1,0:T(4,128)S(1)}, f32[4,2048]{1,0:T(4,128)S(1)}, u32[]{:S(2)}, u32[]{:S(2)}) %collective-permute-start.22) | collective-permute-done | bytes 32800 | tf_op jit(solution)/shard_map/ppermute | solution.py:27
  64.8 1.3 %collective-permute-start.25 = (f32[4,2048]{1,0:T(4,128)S(1)}, f32[4,2048]{1,0:T(4,128)S(1)}, u32[]{:S(2)}, u32[]{:S(2)}) collective-permute-start(f32[4,2048]{1,0:T(4,128)S(1)} %add.92), channel_id=1, source_target_pairs={{0,5},{1,4},{2,7},{3,6},{4,1},{5,0},{6,3},{7,2},{8,13},{9,12},{10,... | collective-permute-start | bytes 98312 | tf_op jit(solution)/shard_map/ppermute | solution.py:27
  66.1 1.8 %collective-permute-start.24 = (f32[4,2048]{1,0:T(4,128)S(1)}, f32[4,2048]{1,0:T(4,128)S(1)}, u32[]{:S(2)}, u32[]{:S(2)}) collective-permute-start(f32[4,2048]{1,0:T(4,128)S(1)} %add.92), channel_id=1, source_target_pairs={{0,12},{1,13},{2,14},{3,15},{4,8},{5,9},{6,10},{7,11},{8,4},{9,5},... | collective-permute-start | bytes 98312 | tf_op jit(solution)/shard_map/ppermute | solution.py:27
  68.0 1.0 %collective-permute-start.23 = (f32[4,2048]{1,0:T(4,128)S(1)}, f32[4,2048]{1,0:T(4,128)S(1)}, u32[]{:S(2)}, u32[]{:S(2)}) collective-permute-start(f32[4,2048]{1,0:T(4,128)S(1)} %add.92), channel_id=1, source_target_pairs={{0,9},{1,8},{2,11},{3,10},{4,13},{5,12},{6,15},{7,14},{8,1},{9,0},... | collective-permute-start | bytes 98312 | tf_op jit(solution)/shard_map/ppermute | solution.py:27
  69.0 0.4 residual.1.refs_1_
  69.4 1.9 %collective-permute-done.25 = f32[4,2048]{1,0:T(4,128)S(1)} collective-permute-done((f32[4,2048]{1,0:T(4,128)S(1)}, f32[4,2048]{1,0:T(4,128)S(1)}, u32[]{:S(2)}, u32[]{:S(2)}) %collective-permute-start.25) | collective-permute-done | bytes 32800 | tf_op jit(solution)/shard_map/ppermute | solution.py:27
  71.3 0.5 collective-permute-done.24
  71.8 0.0 collective-permute-done.23
  71.8 0.4 backward0.1
  72.2 9.2 %all_to_all.11.partial_ref = f32[8,4,128]{2,1,0:T(4,128)S(1)} all-to-all(f32[8,4,128]{2,1,0:T(4,128)S(1)} %get-tuple-element.42), channel_id=1, replica_groups=mesh['leaf'=4,'blk'=8] {'blk'}, dimensions={0} | all-to-all | bytes 32768 | tf_op jit(solution)/shard_map/all_to_all | solution.py:368
  81.5 0.6 closing.1
  (12 shorter events, 0.2 us)
Async XLA Ops:
  16.0 1.3 %collective-permute-start = (f32[4,2048]{1,0:T(4,128)S(1)}, f32[4,2048]{1,0:T(4,128)S(1)}, u32[]{:S(2)}, u32[]{:S(2)}) collective-permute-start(f32[4,2048]{1,0:T(4,128)S(1)} %get-tuple-element.29), channel_id=1, source_target_pairs={{0,8},{1,9},{2,10},{3,11},{4,12},{5,13},{6,14},{7,15},{8,0},{9,1},... | collective-permute-start | bytes 98312 | tf_op jit(solution)/shard_map/ppermute | solution.py:27
  17.3 3.4 %collective-permute-start.1 = (f32[4,2048]{1,0:T(4,128)S(1)}, f32[4,2048]{1,0:T(4,128)S(1)}, u32[]{:S(2)}, u32[]{:S(2)}) collective-permute-start(f32[4,2048]{1,0:T(4,128)S(1)} %add.72), channel_id=1, source_target_pairs={{0,10},{1,11},{2,8},{3,9},{4,14},{5,15},{6,12},{7,13},{8,2},{9,3},... | collective-permute-start | bytes 98312 | tf_op jit(solution)/shard_map/ppermute | solution.py:27
  20.7 7.1 %collective-permute-start.4 = (f32[4,2048]{1,0:T(4,128)S(1)}, f32[4,2048]{1,0:T(4,128)S(1)}, u32[]{:S(2)}, u32[]{:S(2)}) collective-permute-start(f32[4,2048]{1,0:T(4,128)S(1)} %add.73), channel_id=1, source_target_pairs={{0,5},{1,4},{2,7},{3,6},{4,1},{5,0},{6,3},{7,2},{8,13},{9,12},{10,... | collective-permute-start | bytes 98312 | tf_op jit(solution)/shard_map/ppermute | solution.py:27
  21.2 6.5 %collective-permute-start.3 = (f32[4,2048]{1,0:T(4,128)S(1)}, f32[4,2048]{1,0:T(4,128)S(1)}, u32[]{:S(2)}, u32[]{:S(2)}) collective-permute-start(f32[4,2048]{1,0:T(4,128)S(1)} %add.73), channel_id=1, source_target_pairs={{0,12},{1,13},{2,14},{3,15},{4,8},{5,9},{6,10},{7,11},{8,4},{9,5},... | collective-permute-start | bytes 98312 | tf_op jit(solution)/shard_map/ppermute | solution.py:27
  23.1 4.7 %collective-permute-start.2 = (f32[4,2048]{1,0:T(4,128)S(1)}, f32[4,2048]{1,0:T(4,128)S(1)}, u32[]{:S(2)}, u32[]{:S(2)}) collective-permute-start(f32[4,2048]{1,0:T(4,128)S(1)} %add.73), channel_id=1, source_target_pairs={{0,9},{1,8},{2,11},{3,10},{4,13},{5,12},{6,15},{7,14},{8,1},{9,0},... | collective-permute-start | bytes 98312 | tf_op jit(solution)/shard_map/ppermute | solution.py:27
  28.6 1.3 %collective-permute-start.5 = (f32[4,2048]{1,0:T(4,128)S(1)}, f32[4,2048]{1,0:T(4,128)S(1)}, u32[]{:S(2)}, u32[]{:S(2)}) collective-permute-start(f32[4,2048]{1,0:T(4,128)S(1)} %get-tuple-element.35), channel_id=1, source_target_pairs={{0,8},{1,9},{2,10},{3,11},{4,12},{5,13},{6,14},{7,15},{8,0},{9,1},... | collective-permute-start | bytes 98312 | tf_op jit(solution)/shard_map/ppermute | solution.py:27
  29.8 4.9 %collective-permute-start.8 = (f32[4,2048]{1,0:T(4,128)S(1)}, f32[4,2048]{1,0:T(4,128)S(1)}, u32[]{:S(2)}, u32[]{:S(2)}) collective-permute-start(f32[4,2048]{1,0:T(4,128)S(1)} %add.77), channel_id=1, source_target_pairs={{0,17},{1,16},{2,19},{3,18},{4,21},{5,20},{6,23},{7,22},{8,25},{9,... | collective-permute-start | bytes 98312 | tf_op jit(solution)/shard_map/ppermute | solution.py:27
  31.4 4.0 %collective-permute-start.7 = (f32[4,2048]{1,0:T(4,128)S(1)}, f32[4,2048]{1,0:T(4,128)S(1)}, u32[]{:S(2)}, u32[]{:S(2)}) collective-permute-start(f32[4,2048]{1,0:T(4,128)S(1)} %add.77), channel_id=1, source_target_pairs={{0,9},{1,8},{2,11},{3,10},{4,13},{5,12},{6,15},{7,14},{8,1},{9,0},... | collective-permute-start | bytes 98312 | tf_op jit(solution)/shard_map/ppermute | solution.py:27
  32.4 3.3 %collective-permute-start.6 = (f32[4,2048]{1,0:T(4,128)S(1)}, f32[4,2048]{1,0:T(4,128)S(1)}, u32[]{:S(2)}, u32[]{:S(2)}) collective-permute-start(f32[4,2048]{1,0:T(4,128)S(1)} %add.77), channel_id=1, source_target_pairs={{0,24},{1,25},{2,26},{3,27},{4,28},{5,29},{6,30},{7,31},{8,16},{9,... | collective-permute-start | bytes 98312 | tf_op jit(solution)/shard_map/ppermute | solution.py:27
  35.7 6.2 %collective-permute-start.11 = (f32[4,2048]{1,0:T(4,128)S(1)}, f32[4,2048]{1,0:T(4,128)S(1)}, u32[]{:S(2)}, u32[]{:S(2)}) collective-permute-start(f32[4,2048]{1,0:T(4,128)S(1)} %add_add_fusion.4), channel_id=1, source_target_pairs={{0,6},{1,7},{2,4},{3,5},{4,2},{5,3},{6,0},{7,1},{8,14},{9,15},{10,... | collective-permute-start | bytes 98312 | tf_op jit(solution)/shard_map/ppermute | solution.py:27
  36.4 5.6 %collective-permute-start.10 = (f32[4,2048]{1,0:T(4,128)S(1)}, f32[4,2048]{1,0:T(4,128)S(1)}, u32[]{:S(2)}, u32[]{:S(2)}) collective-permute-start(f32[4,2048]{1,0:T(4,128)S(1)} %add_add_fusion.4), channel_id=1, source_target_pairs={{0,12},{1,13},{2,14},{3,15},{4,8},{5,9},{6,10},{7,11},{8,4},{9,5},... | collective-permute-start | bytes 98312 | tf_op jit(solution)/shard_map/ppermute | solution.py:27
  37.1 5.1 %collective-permute-start.9 = (f32[4,2048]{1,0:T(4,128)S(1)}, f32[4,2048]{1,0:T(4,128)S(1)}, u32[]{:S(2)}, u32[]{:S(2)}) collective-permute-start(f32[4,2048]{1,0:T(4,128)S(1)} %add_add_fusion.4), channel_id=1, source_target_pairs={{0,10},{1,11},{2,8},{3,9},{4,14},{5,15},{6,12},{7,13},{8,2},{9,3},... | collective-permute-start | bytes 98312 | tf_op jit(solution)/shard_map/ppermute | solution.py:27
  42.2 1.3 %collective-permute-start.12 = (f32[4,2048]{1,0:T(4,128)S(1)}, f32[4,2048]{1,0:T(4,128)S(1)}, u32[]{:S(2)}, u32[]{:S(2)}) collective-permute-start(f32[4,2048]{1,0:T(4,128)S(1)} %add_add_fusion.3.refs_0_), channel_id=1, source_target_pairs={{0,8},{1,9},{2,10},{3,11},{4,12},{5,13},{6,14},{7,15},{8,0},{9,1},... | collective-permute-start | bytes 98312 | tf_op jit(solution)/shard_map/ppermute | solution.py:27
  44.4 1.3 %collective-permute-start.13 = (f32[4,2048]{1,0:T(4,128)S(1)}, f32[4,2048]{1,0:T(4,128)S(1)}, u32[]{:S(2)}, u32[]{:S(2)}) collective-permute-start(f32[4,2048]{1,0:T(4,128)S(1)} %get-tuple-element.38), channel_id=1, source_target_pairs={{0,8},{1,9},{2,10},{3,11},{4,12},{5,13},{6,14},{7,15},{8,0},{9,1},... | collective-permute-start | bytes 98312 | tf_op jit(solution)/shard_map/ppermute | solution.py:27
  45.6 4.9 %collective-permute-start.16 = (f32[4,2048]{1,0:T(4,128)S(1)}, f32[4,2048]{1,0:T(4,128)S(1)}, u32[]{:S(2)}, u32[]{:S(2)}) collective-permute-start(f32[4,2048]{1,0:T(4,128)S(1)} %add.84), channel_id=1, source_target_pairs={{0,17},{1,16},{2,19},{3,18},{4,21},{5,20},{6,23},{7,22},{8,25},{9,... | collective-permute-start | bytes 98312 | tf_op jit(solution)/shard_map/ppermute | solution.py:27
  47.4 3.8 %collective-permute-start.15 = (f32[4,2048]{1,0:T(4,128)S(1)}, f32[4,2048]{1,0:T(4,128)S(1)}, u32[]{:S(2)}, u32[]{:S(2)}) collective-permute-start(f32[4,2048]{1,0:T(4,128)S(1)} %add.84), channel_id=1, source_target_pairs={{0,9},{1,8},{2,11},{3,10},{4,13},{5,12},{6,15},{7,14},{8,1},{9,0},... | collective-permute-start | bytes 98312 | tf_op jit(solution)/shard_map/ppermute | solution.py:27
  47.6 3.6 %collective-permute-start.14 = (f32[4,2048]{1,0:T(4,128)S(1)}, f32[4,2048]{1,0:T(4,128)S(1)}, u32[]{:S(2)}, u32[]{:S(2)}) collective-permute-start(f32[4,2048]{1,0:T(4,128)S(1)} %add.84), channel_id=1, source_target_pairs={{0,24},{1,25},{2,26},{3,27},{4,28},{5,29},{6,30},{7,31},{8,16},{9,... | collective-permute-start | bytes 98312 | tf_op jit(solution)/shard_map/ppermute | solution.py:27
  51.2 6.0 %collective-permute-start.19 = (f32[4,2048]{1,0:T(4,128)S(1)}, f32[4,2048]{1,0:T(4,128)S(1)}, u32[]{:S(2)}, u32[]{:S(2)}) collective-permute-start(f32[4,2048]{1,0:T(4,128)S(1)} %add_add_fusion.2), channel_id=1, source_target_pairs={{0,6},{1,7},{2,4},{3,5},{4,2},{5,3},{6,0},{7,1},{8,14},{9,15},{10,... | collective-permute-start | bytes 98312 | tf_op jit(solution)/shard_map/ppermute | solution.py:27
  52.9 5.3 %collective-permute-start.18 = (f32[4,2048]{1,0:T(4,128)S(1)}, f32[4,2048]{1,0:T(4,128)S(1)}, u32[]{:S(2)}, u32[]{:S(2)}) collective-permute-start(f32[4,2048]{1,0:T(4,128)S(1)} %add_add_fusion.2), channel_id=1, source_target_pairs={{0,12},{1,13},{2,14},{3,15},{4,8},{5,9},{6,10},{7,11},{8,4},{9,5},... | collective-permute-start | bytes 98312 | tf_op jit(solution)/shard_map/ppermute | solution.py:27
  53.4 4.8 %collective-permute-start.17 = (f32[4,2048]{1,0:T(4,128)S(1)}, f32[4,2048]{1,0:T(4,128)S(1)}, u32[]{:S(2)}, u32[]{:S(2)}) collective-permute-start(f32[4,2048]{1,0:T(4,128)S(1)} %add_add_fusion.2), channel_id=1, source_target_pairs={{0,10},{1,11},{2,8},{3,9},{4,14},{5,15},{6,12},{7,13},{8,2},{9,3},... | collective-permute-start | bytes 98312 | tf_op jit(solution)/shard_map/ppermute | solution.py:27
  58.2 1.3 %collective-permute-start.20 = (f32[4,2048]{1,0:T(4,128)S(1)}, f32[4,2048]{1,0:T(4,128)S(1)}, u32[]{:S(2)}, u32[]{:S(2)}) collective-permute-start(f32[4,2048]{1,0:T(4,128)S(1)} %add_add_fusion.1.refs_0_), channel_id=1, source_target_pairs={{0,8},{1,9},{2,10},{3,11},{4,12},{5,13},{6,14},{7,15},{8,0},{9,1},... | collective-permute-start | bytes 98312 | tf_op jit(solution)/shard_map/ppermute | solution.py:27
  60.1 1.3 %collective-permute-start.21 = (f32[4,2048]{1,0:T(4,128)S(1)}, f32[4,2048]{1,0:T(4,128)S(1)}, u32[]{:S(2)}, u32[]{:S(2)}) collective-permute-start(f32[4,2048]{1,0:T(4,128)S(1)} %get-tuple-element.40), channel_id=1, source_target_pairs={{0,8},{1,9},{2,10},{3,11},{4,12},{5,13},{6,14},{7,15},{8,0},{9,1},... | collective-permute-start | bytes 98312 | tf_op jit(solution)/shard_map/ppermute | solution.py:27
  61.4 3.4 %collective-permute-start.22 = (f32[4,2048]{1,0:T(4,128)S(1)}, f32[4,2048]{1,0:T(4,128)S(1)}, u32[]{:S(2)}, u32[]{:S(2)}) collective-permute-start(f32[4,2048]{1,0:T(4,128)S(1)} %add.91), channel_id=1, source_target_pairs={{0,10},{1,11},{2,8},{3,9},{4,14},{5,15},{6,12},{7,13},{8,2},{9,3},... | collective-permute-start | bytes 98312 | tf_op jit(solution)/shard_map/ppermute | solution.py:27
  64.8 6.5 %collective-permute-start.25 = (f32[4,2048]{1,0:T(4,128)S(1)}, f32[4,2048]{1,0:T(4,128)S(1)}, u32[]{:S(2)}, u32[]{:S(2)}) collective-permute-start(f32[4,2048]{1,0:T(4,128)S(1)} %add.92), channel_id=1, source_target_pairs={{0,5},{1,4},{2,7},{3,6},{4,1},{5,0},{6,3},{7,2},{8,13},{9,12},{10,... | collective-permute-start | bytes 98312 | tf_op jit(solution)/shard_map/ppermute | solution.py:27
  66.1 5.6 %collective-permute-start.24 = (f32[4,2048]{1,0:T(4,128)S(1)}, f32[4,2048]{1,0:T(4,128)S(1)}, u32[]{:S(2)}, u32[]{:S(2)}) collective-permute-start(f32[4,2048]{1,0:T(4,128)S(1)} %add.92), channel_id=1, source_target_pairs={{0,12},{1,13},{2,14},{3,15},{4,8},{5,9},{6,10},{7,11},{8,4},{9,5},... | collective-permute-start | bytes 98312 | tf_op jit(solution)/shard_map/ppermute | solution.py:27
  68.0 3.8 %collective-permute-start.23 = (f32[4,2048]{1,0:T(4,128)S(1)}, f32[4,2048]{1,0:T(4,128)S(1)}, u32[]{:S(2)}, u32[]{:S(2)}) collective-permute-start(f32[4,2048]{1,0:T(4,128)S(1)} %add.92), channel_id=1, source_target_pairs={{0,9},{1,8},{2,11},{3,10},{4,13},{5,12},{6,15},{7,14},{8,1},{9,0},... | collective-permute-start | bytes 98312 | tf_op jit(solution)/shard_map/ppermute | solution.py:27
